TPU v7x, 32 devices: a whole 2x2x4 slice. The times are simulated.
32 devices in a mesh: dp: 2 (over x), pp: 4 (over z), ep: 4 (over y, core).
Axes of the slice: x: 2, y: 2, z: 4, core: 2. Of those that a mesh axis runs over, the one named last changes fastest.
Arguments:
- x_a: bfloat16 [8, 4, 128, 768], P(('dp', 'pp'), 'ep'), parts along dimension 0
- x_b: bfloat16 [8, 4, 128, 768], P(('dp', 'pp'), 'ep'), parts along dimension 0
- g_b: bfloat16 [8, 4, 128, 768], P(('dp', 'pp'), 'ep'), parts along dimension 0
- ids_a: int32 [8, 4, 128, 2], P(('dp', 'pp'), 'ep'), parts along dimension 0
- ids_b: int32 [8, 4, 128, 2], P(('dp', 'pp'), 'ep'), parts along dimension 0
- count_a: int32 [8, 4, 8], P(('dp', 'pp'), 'ep'), parts along dimension 0
- count_b: int32 [8, 4, 8], P(('dp', 'pp'), 'ep'), parts along dimension 0
- gain_1: bfloat16 [4, 768], P('pp')
- gain_2: bfloat16 [4, 768], P('pp')
- w_q: bfloat16 [4, 768, 6, 128], P('pp')
- w_k: bfloat16 [4, 768, 1, 128], P('pp')
- w_v: bfloat16 [4, 768, 1, 128], P('pp')
- w_o: bfloat16 [4, 6, 128, 768], P('pp')
- w_r: bfloat16 [4, 768, 8], P('pp')
- w_1: bfloat16 [4, 8, 768, 2048], P('pp', 'ep')
- w_3: bfloat16 [4, 8, 768, 2048], P('pp', 'ep')
- w_2: bfloat16 [4, 8, 2048, 768], P('pp', 'ep')
Outputs:
- output 1: bfloat16 [8, 4, 128, 768], P(('dp', 'pp'), 'ep'), parts along dimension 0
- output 2: bfloat16 [8, 4, 128, 768], P(('dp', 'pp'), 'ep'), parts along dimension 0
- output 3: float32 [8, 768], P(('dp', 'pp')), parts along dimension 0
- output 4: float32 [8, 768], P(('dp', 'pp')), parts along dimension 0
- output 5: float32 [8, 768, 6, 128], P(('dp', 'pp')), parts along dimension 0
- output 6: float32 [8, 768, 1, 128], P(('dp', 'pp')), parts along dimension 0
- output 7: float32 [8, 768, 1, 128], P(('dp', 'pp')), parts along dimension 0
- output 8: float32 [8, 6, 128, 768], P(('dp', 'pp')), parts along dimension 0
- output 9: float32 [8, 768, 8], P(('dp', 'pp')), parts along dimension 0
- output 10: float32 [8, 8, 768, 2048], P(('dp', 'pp'), 'ep'), parts along dimension 0
- output 11: float32 [8, 8, 768, 2048], P(('dp', 'pp'), 'ep'), parts along dimension 0
- output 12: float32 [8, 8, 2048, 768], P(('dp', 'pp'), 'ep'), parts along dimension 0
There are 2 independent parts. A program takes and returns all parts, laid end to end along the dimension named above; an argument that names none is the same for every part.
All inputs are finite; a program needn't handle non-finite values.
Results may differ from a plain program's by a relative error of at most 0.019921.
Values are sent between devices in bfloat16 or wider.
A program may use at most 1 GiB of HBM per device.

v0:
```python
import jax
import jax.numpy as jnp
from jax import lax
from jax.sharding import PartitionSpec as P

NORM_EPS = 1e-6
LOAD_FACTOR = 4
MASK_VALUE = -1e30


def rms_scale(x_f32, gain):
    inv_rms = lax.rsqrt(jnp.mean(x_f32 * x_f32, axis=-1, keepdims=True) + NORM_EPS)
    normed = (x_f32 * inv_rms * gain.astype(jnp.float32)).astype(jnp.bfloat16)
    return normed, inv_rms


def rms_back(x_f32, inv_rms, gain, d_normed):
    x_hat = x_f32 * inv_rms
    d_gain = jnp.sum((d_normed * x_hat).reshape(-1, x_f32.shape[-1]), axis=0)
    d_hat = d_normed * gain.astype(jnp.float32)
    d_input = inv_rms * (d_hat - x_hat * jnp.mean(d_hat * x_hat, axis=-1, keepdims=True))
    return d_input, d_gain


def attention_forward(x_seq, gain_1, w_q, w_k, w_v, w_o):
    seq_len, d_model = x_seq.shape[1], x_seq.shape[2]
    kv_heads, head_dim = w_k.shape[1], w_k.shape[2]
    group_rep = w_q.shape[1] // kv_heads
    x_f32 = x_seq.astype(jnp.float32)
    normed, inv_rms = rms_scale(x_f32, gain_1)
    wq_grp = w_q.reshape(d_model, kv_heads, group_rep, head_dim)
    query_bf = jnp.einsum('nsd,dgrk->nsgrk', normed, wq_grp, preferred_element_type=jnp.float32).astype(jnp.bfloat16)
    key_bf = jnp.einsum('nsd,dgk->nsgk', normed, w_k, preferred_element_type=jnp.float32).astype(jnp.bfloat16)
    value_bf = jnp.einsum('nsd,dgk->nsgk', normed, w_v, preferred_element_type=jnp.float32).astype(jnp.bfloat16)
    scores = jnp.einsum('nsgrk,ntgk->ngrst', query_bf, key_bf, preferred_element_type=jnp.float32) * head_dim ** -0.5
    causal = jnp.arange(seq_len)[:, None] >= jnp.arange(seq_len)[None, :]
    probs_f32 = jax.nn.softmax(jnp.where(causal, scores, MASK_VALUE), axis=-1)
    probs_bf = probs_f32.astype(jnp.bfloat16)
    attn_out = jnp.einsum('ngrst,ntgk->nsgrk', probs_bf, value_bf, preferred_element_type=jnp.float32).astype(jnp.bfloat16)
    wo_grp = w_o.reshape(kv_heads, group_rep, head_dim, d_model)
    attn_proj = jnp.einsum('nsgrk,grkd->nsd', attn_out, wo_grp, preferred_element_type=jnp.float32)
    hidden = (x_f32 + attn_proj).astype(jnp.bfloat16)
    saved_fwd = (x_f32, inv_rms, normed, query_bf, key_bf, value_bf, probs_f32, probs_bf, attn_out)
    return hidden, saved_fwd


def attention_backward(d_hidden, saved_fwd, gain_1, w_q, w_k, w_v, w_o):
    x_f32, inv_rms, normed, query_bf, key_bf, value_bf, probs_f32, probs_bf, attn_out = saved_fwd
    d_model = x_f32.shape[-1]
    kv_heads, head_dim = w_k.shape[1], w_k.shape[2]
    group_rep = w_q.shape[1] // kv_heads
    wq_grp = w_q.reshape(d_model, kv_heads, group_rep, head_dim)
    wo_grp = w_o.reshape(kv_heads, group_rep, head_dim, d_model)
    d_hid_bf = d_hidden.astype(jnp.bfloat16)
    d_w_o = jnp.einsum('nsgrk,nsd->grkd', attn_out, d_hid_bf, preferred_element_type=jnp.float32).reshape(w_o.shape)
    d_attn = jnp.einsum('nsd,grkd->nsgrk', d_hid_bf, wo_grp, preferred_element_type=jnp.float32).astype(jnp.bfloat16)
    d_probs = jnp.einsum('nsgrk,ntgk->ngrst', d_attn, value_bf, preferred_element_type=jnp.float32)
    d_value = jnp.einsum('ngrst,nsgrk->ntgk', probs_bf, d_attn, preferred_element_type=jnp.float32).astype(jnp.bfloat16)
    d_scores = (probs_f32 * (d_probs - jnp.sum(probs_f32 * d_probs, axis=-1, keepdims=True)) * head_dim ** -0.5).astype(jnp.bfloat16)
    d_query = jnp.einsum('ngrst,ntgk->nsgrk', d_scores, key_bf, preferred_element_type=jnp.float32).astype(jnp.bfloat16)
    d_key = jnp.einsum('ngrst,nsgrk->ntgk', d_scores, query_bf, preferred_element_type=jnp.float32).astype(jnp.bfloat16)
    d_w_q = jnp.einsum('nsd,nsgrk->dgrk', normed, d_query, preferred_element_type=jnp.float32).reshape(w_q.shape)
    d_w_k = jnp.einsum('nsd,nsgk->dgk', normed, d_key, preferred_element_type=jnp.float32)
    d_w_v = jnp.einsum('nsd,nsgk->dgk', normed, d_value, preferred_element_type=jnp.float32)
    d_normed = (jnp.einsum('nsgrk,dgrk->nsd', d_query, wq_grp, preferred_element_type=jnp.float32)
                + jnp.einsum('nsgk,dgk->nsd', d_key, w_k, preferred_element_type=jnp.float32)
                + jnp.einsum('nsgk,dgk->nsd', d_value, w_v, preferred_element_type=jnp.float32))
    d_input, d_gain = rms_back(x_f32, inv_rms, gain_1, d_normed)
    return d_input + d_hidden, d_gain, d_w_q, d_w_k, d_w_v, d_w_o


def routing_plan(ids_flat, counts, num_experts, capacity):
    n_choice = ids_flat.shape[0]
    onehot = (ids_flat[:, None] == jnp.arange(num_experts)[None, :]).astype(jnp.int32)
    rank_idx = jnp.sum(onehot * (jnp.cumsum(onehot, axis=0) - 1), axis=1)
    keep_mask = rank_idx < counts[ids_flat]
    slot_idx = jnp.where(keep_mask, ids_flat * capacity + rank_idx, num_experts * capacity)
    choice_idx = jnp.zeros((num_experts * capacity,), jnp.int32).at[slot_idx].set(jnp.arange(n_choice, dtype=jnp.int32), mode='drop')
    slot_live = jnp.zeros((num_experts * capacity,), jnp.int32).at[slot_idx].set(1, mode='drop') > 0
    return onehot, keep_mask, slot_idx, choice_idx, slot_live


def moe_forward(hidden, route_ids, counts, gain_2, w_r, w_1, w_3, w_2, exchange):
    seq_count, seq_len, d_model = hidden.shape
    tok_dev = seq_count * seq_len
    top_k = route_ids.shape[-1]
    num_experts = w_r.shape[1]
    e_local = w_1.shape[0]
    ep_size = num_experts // e_local
    capacity = min(tok_dev, LOAD_FACTOR * tok_dev * top_k // num_experts)
    hid_f32 = hidden.reshape(tok_dev, d_model).astype(jnp.float32)
    normed, inv_rms = rms_scale(hid_f32, gain_2)
    logits = jnp.dot(normed, w_r, preferred_element_type=jnp.float32)
    onehot, keep_mask, slot_idx, choice_idx, slot_live = routing_plan(route_ids.reshape(-1), counts, num_experts, capacity)
    chosen = onehot.reshape(tok_dev, top_k, num_experts) > 0
    gate_w = jax.nn.softmax(jnp.sum(jnp.where(chosen, logits[:, None, :], 0.0), axis=-1), axis=-1)
    send_buf = jnp.where(slot_live[:, None], jnp.take(normed, choice_idx // top_k, axis=0), jnp.zeros((), jnp.bfloat16))
    recv_buf = exchange(send_buf.reshape(ep_size, e_local, capacity, d_model))
    gate_pre = jnp.einsum('secd,edf->secf', recv_buf, w_1, preferred_element_type=jnp.float32)
    up_pre = jnp.einsum('secd,edf->secf', recv_buf, w_3, preferred_element_type=jnp.float32)
    act_bf = (jax.nn.silu(gate_pre) * up_pre).astype(jnp.bfloat16)
    expert_out = jnp.einsum('secf,efd->secd', act_bf, w_2, preferred_element_type=jnp.float32).astype(jnp.bfloat16)
    back_buf = exchange(expert_out).reshape(num_experts * capacity, d_model)
    picked = jnp.take(back_buf, slot_idx, axis=0, mode='clip').reshape(tok_dev, top_k, d_model)
    keep_tk = keep_mask.reshape(tok_dev, top_k)
    weight = jnp.where(keep_tk, gate_w, 0.0)
    combined = jnp.sum(weight[:, :, None] * picked.astype(jnp.float32), axis=1)
    y_out = (hid_f32 + combined).astype(jnp.bfloat16).reshape(seq_count, seq_len, d_model)
    saved_fwd = (hid_f32, inv_rms, normed, chosen, gate_w, keep_tk, slot_idx, choice_idx, slot_live, recv_buf, gate_pre, up_pre, act_bf, picked)
    return y_out, saved_fwd


def moe_backward(d_out, saved_fwd, gain_2, w_r, w_1, w_3, w_2, exchange):
    hid_f32, inv_rms, normed, chosen, gate_w, keep_tk, slot_idx, choice_idx, slot_live, recv_buf, gate_pre, up_pre, act_bf, picked = saved_fwd
    top_k = gate_w.shape[1]
    d_model = hid_f32.shape[-1]
    num_experts = w_r.shape[1]
    e_local = w_1.shape[0]
    ep_size = num_experts // e_local
    capacity = recv_buf.shape[2]
    weight = jnp.where(keep_tk, gate_w, 0.0)
    d_gate = jnp.where(keep_tk, jnp.sum(picked.astype(jnp.float32) * d_out[:, None, :], axis=-1), 0.0)
    d_sel = gate_w * (d_gate - jnp.sum(gate_w * d_gate, axis=-1, keepdims=True))
    d_logits = jnp.sum(jnp.where(chosen, d_sel[:, :, None], 0.0), axis=1).astype(jnp.bfloat16)
    slot_gate = jnp.where(slot_live, jnp.take(weight.reshape(-1), choice_idx), 0.0)
    d_back = (jnp.take(d_out, choice_idx // top_k, axis=0) * slot_gate[:, None]).astype(jnp.bfloat16)
    d_expert = exchange(d_back.reshape(ep_size, e_local, capacity, d_model))
    d_act = jnp.einsum('secd,efd->secf', d_expert, w_2, preferred_element_type=jnp.float32)
    d_w_2 = jnp.einsum('secf,secd->efd', act_bf, d_expert, preferred_element_type=jnp.float32)
    sig_gate = jax.nn.sigmoid(gate_pre)
    d_act_f32 = d_act.astype(jnp.bfloat16).astype(jnp.float32)
    d_up = (d_act_f32 * gate_pre * sig_gate).astype(jnp.bfloat16)
    d_gate_pre = (d_act_f32 * up_pre * sig_gate * (1.0 + gate_pre * (1.0 - sig_gate))).astype(jnp.bfloat16)
    d_w_1 = jnp.einsum('secd,secf->edf', recv_buf, d_gate_pre, preferred_element_type=jnp.float32)
    d_w_3 = jnp.einsum('secd,secf->edf', recv_buf, d_up, preferred_element_type=jnp.float32)
    d_recv = (jnp.einsum('secf,edf->secd', d_gate_pre, w_1, preferred_element_type=jnp.float32)
              + jnp.einsum('secf,edf->secd', d_up, w_3, preferred_element_type=jnp.float32)).astype(jnp.bfloat16)
    d_send = exchange(d_recv).reshape(num_experts * capacity, d_model)
    d_picked = jnp.take(d_send, slot_idx, axis=0, mode='clip').reshape(gate_w.shape[0], top_k, d_model)
    d_normed = (jnp.sum(jnp.where(keep_tk[:, :, None], d_picked.astype(jnp.float32), 0.0), axis=1)
                + jnp.einsum('te,de->td', d_logits, w_r, preferred_element_type=jnp.float32))
    d_w_r = jnp.einsum('td,te->de', normed, d_logits, preferred_element_type=jnp.float32)
    d_hid, d_gain = rms_back(hid_f32, inv_rms, gain_2, d_normed)
    return d_hid + d_out, d_gain, d_w_r, d_w_1, d_w_3, d_w_2


def solution(mesh):
    pp_size = mesh.shape['pp']
    stage_fwd = [(stage_idx, (stage_idx + 1) % pp_size) for stage_idx in range(pp_size)]
    stage_bwd = [(stage_idx, (stage_idx - 1) % pp_size) for stage_idx in range(pp_size)]

    def exchange(send_block):
        return lax.all_to_all(send_block, 'ep', 0, 0, tiled=True)

    def device_tick(x_a, x_b, g_b, ids_a, ids_b, count_a, count_b, gain_1, gain_2, w_q, w_k, w_v, w_o, w_r, w_1, w_3, w_2):
        attn_w = (gain_1[0], w_q[0], w_k[0], w_v[0], w_o[0])
        moe_w = (gain_2[0], w_r[0], w_1[0], w_3[0], w_2[0])
        seq_count, seq_len, d_model = x_b.shape[1], x_b.shape[2], x_b.shape[3]
        hid_a, _ = attention_forward(x_a[0], *attn_w)
        y_a, _ = moe_forward(hid_a, ids_a[0], count_a[0, 0], *moe_w, exchange)
        hid_b, attn_saved = attention_forward(x_b[0], *attn_w)
        _, moe_saved = moe_forward(hid_b, ids_b[0], count_b[0, 0], *moe_w, exchange)
        d_out = g_b[0].reshape(seq_count * seq_len, d_model).astype(jnp.float32)
        d_hid, d_gain_2, d_w_r, d_w_1, d_w_3, d_w_2 = moe_backward(d_out, moe_saved, *moe_w, exchange)
        d_x, d_gain_1, d_w_q, d_w_k, d_w_v, d_w_o = attention_backward(d_hid.reshape(seq_count, seq_len, d_model), attn_saved, *attn_w)
        dense_sum = lax.psum((d_gain_1, d_gain_2, d_w_q, d_w_k, d_w_v, d_w_o, d_w_r), 'ep')
        y_next = lax.ppermute(y_a, 'pp', stage_fwd)
        dx_prev = lax.ppermute(d_x.astype(jnp.bfloat16), 'pp', stage_bwd)
        return (y_next[None], dx_prev[None]) + tuple(grad_part[None] for grad_part in dense_sum) + (d_w_1[None], d_w_3[None], d_w_2[None])

    tok_spec = P(('dp', 'pp'), 'ep', None, None)
    cnt_spec = P(('dp', 'pp'), 'ep', None)
    gain_spec = P('pp', None)
    attn_spec = P('pp', None, None, None)
    router_spec = P('pp', None, None)
    expert_spec = P('pp', 'ep', None, None)
    gain_out = P(('dp', 'pp'), None)
    attn_out_spec = P(('dp', 'pp'), None, None, None)
    router_out = P(('dp', 'pp'), None, None)
    expert_out_spec = P(('dp', 'pp'), 'ep', None, None)
    in_specs = (tok_spec, tok_spec, tok_spec, tok_spec, tok_spec, cnt_spec, cnt_spec, gain_spec, gain_spec,
                attn_spec, attn_spec, attn_spec, attn_spec, router_spec, expert_spec, expert_spec, expert_spec)
    out_specs = (tok_spec, tok_spec, gain_out, gain_out, attn_out_spec, attn_out_spec, attn_out_spec, attn_out_spec,
                 router_out, expert_out_spec, expert_out_spec, expert_out_spec)
    return jax.shard_map(device_tick, mesh=mesh, in_specs=in_specs, out_specs=out_specs, check_vma=False)
```

profile of v0, /device:TPU:0, one launch (start us, length us, event | category | flops | bytes accessed | tf_op | source)
XLA Modules:
  0.0 401.9 jit_solution(11961223997257969514)
XLA Ops:
  10.2 1.9 fusion.112
  12.1 1.9 fusion.111
  15.2 1.9 fusion.109
  19.1 1.6 fusion.208
  21.6 4.5 %compare_select_fusion.6 = s32[256,1]{0,1:T(1,128)S(1)} fusion(s32[]{:T(128)} %bitcast.66, s32[]{:T(128)} %bitcast.67, s32[]{:T(128)} %bitcast.68, s32[]{:T(128)} %bitcast.69, s32[]{:T(128)} %bitcast.70, s32[]{:T(128)} %bitcast.72, s32[]{:T(128)} %bitcast.71, s32[256,1]{0,1:T(1,128)S(1)} %reshape_squeeze.5), kind=kLoop, calls=%fused_computation.250 | loop fusion | flops 3840 | bytes 2076 | tf_op jit(solution)/shard_map/gather | solution.py:76
  29.4 1.4 scatter_custom_fusion.3
  39.7 2.9 multiply_reduce_fusion.6
  44.4 5.2 %gather_fusion.6 = bf16[1024,768]{1,0:T(8,128)(2,1)} fusion(bf16[128,768]{1,0:T(8,128)(2,1)S(1)} %multiply_convert_fusion.2, s32[1024]{0:T(1024)S(1)} %get-tuple-element.99), kind=kCustom, calls=%fused_computation.1.clone | custom fusion | bytes 3149824 | tf_op jit(solution)/shard_map/jit(_take)/gather | solution.py:97
  49.6 2.9 select_select_fusion
  52.5 4.8 %all-to-all-start.3 = ((bf16[4,2,128,768]{3,2,1,0:T(8,128)(2,1)}), bf16[4,2,128,768]{3,2,1,0:T(8,128)(2,1)S(1)}, u32[]{:S(2)}, u32[]{:S(2)}) async-start(bf16[4,2,128,768]{3,2,1,0:T(8,128)(2,1)} %bitcast.478), calls=%async_computation.3 | async-start | bytes 3145728 | tf_op jit(solution)/shard_map/all_to_all | solution.py:153
  60.5 16.6 %all-to-all-done.3 = bf16[4,2,128,768]{3,2,1,0:T(8,128)(2,1)S(1)} async-done(((bf16[4,2,128,768]{3,2,1,0:T(8,128)(2,1)}), bf16[4,2,128,768]{3,2,1,0:T(8,128)(2,1)S(1)}, u32[]{:S(2)}, u32[]{:S(2)}) %all-to-all-start.3) | async-done | bytes 1572896 | tf_op jit(solution)/shard_map/all_to_all | solution.py:153
  77.1 5.7 %fusion.23 = f32[2,4,128,2048]{3,2,1,0:T(8,128)S(1)} fusion(bf16[1,2,768,2048]{3,2,1,0:T(8,128)(2,1)} %param.34, bf16[4,2,128,768]{3,2,1,0:T(8,128)(2,1)S(1)} %all-to-all-done.3), kind=kOutput, calls=%fused_computation.42 | convolution fusion | flops 3221225472 | bytes 16252928 | tf_op jit(solution)/shard_map/secd,edf->secf/dot_general | solution.py:100
  82.8 12.3 %fusion.9 = (bf16[4,2,128,2048]{3,2,0,1:T(8,128)(2,1)S(1)}, f32[2,4,128,2048]{3,2,1,0:T(8,128)}) fusion(f32[2,4,128,2048]{3,2,1,0:T(8,128)S(1)} %fusion.23, bf16[1,2,768,2048]{3,2,1,0:T(8,128)(2,1)} %param.33, bf16[4,2,128,768]{3,2,1,0:T(8,128)(2,1)S(1)} %all-to-all-done.3), kind=kOutput, calls=%fused_computation.24 | convolution fusion | flops 3233808384 | bytes 28835840 | tf_op jit(solution)/shard_map/secd,edf->secf/dot_general | solution.py:99
  95.1 3.5 fusion.49
  99.8 4.4 %all-to-all-start.5 = ((bf16[4,2,128,768]{3,2,1,0:T(8,128)(2,1)}), bf16[4,2,128,768]{3,2,1,0:T(8,128)(2,1)}, u32[]{:S(2)}, u32[]{:S(2)}) async-start(bf16[4,2,128,768]{3,2,1,0:T(8,128)(2,1)} %copy.191), calls=%async_computation.5 | async-start | bytes 3145728 | tf_op jit(solution)/shard_map/all_to_all | solution.py:153
  104.2 1.5 slice_reduce_fusion.1
  105.7 1.6 reshape_squeeze.4
  107.3 1.6 eq.68
  115.3 5.5 %gather_fusion.1 = f32[1024,768]{1,0:T(8,128)} fusion(f32[128,768]{1,0:T(8,128)S(1)} %bitcast_convert_fusion, s32[1024]{0:T(1024)} %copy-done.39), kind=kCustom, calls=%fused_computation.3 | custom fusion | bytes 6295552 | tf_op jit(solution)/shard_map/jit(_take)/gather | solution.py:126
  126.4 1.6 fusion.209
  128.8 5.0 %compare_select_fusion.12 = s32[256,1]{0,1:T(1,128)S(1)} fusion(s32[]{:T(128)} %bitcast.19, s32[]{:T(128)} %bitcast.20, s32[]{:T(128)} %bitcast.21, s32[]{:T(128)} %bitcast.22, s32[]{:T(128)} %bitcast.23, s32[]{:T(128)} %bitcast.25, s32[]{:T(128)} %bitcast.24, s32[256,1]{0,1:T(1,128)} %reshape_squeeze.4), kind=kLoop, calls=%fused_computation.257 | loop fusion | flops 3840 | bytes 2076 | tf_op jit(solution)/shard_map/gather | solution.py:76
  135.0 3.9 gather_fusion.4
  138.9 2.3 reshape.1002
  141.1 2.2 multiply_reduce_fusion
  145.9 6.9 %gather_fusion.2 = f32[1024]{0:T(1024)S(1)} fusion(f32[256]{0:T(256)S(1)} %broadcast_select_fusion.2, s32[1024]{0:T(1024)} %get-tuple-element.98), kind=kCustom, calls=%fused_computation.4 | custom fusion | bytes 12288 | tf_op jit(solution)/shard_map/jit(_take)/gather | solution.py:125
  153.0 3.4 multiply_convert_fusion
  156.4 4.4 %all-to-all-start.2 = ((bf16[4,2,128,768]{3,2,1,0:T(8,128)(2,1)}), bf16[4,2,128,768]{3,2,1,0:T(8,128)(2,1)}, u32[]{:S(2)}, u32[]{:S(2)}) async-start(bf16[4,2,128,768]{3,2,1,0:T(8,128)(2,1)} %multiply_convert_fusion), calls=%async_computation.2 | async-start | bytes 3145728 | tf_op jit(solution)/shard_map/all_to_all | solution.py:153
  160.8 1.7 scatter_custom_fusion
  162.5 1.4 scatter_custom_fusion.1
  167.4 13.2 %all-to-all-done.2 = bf16[4,2,128,768]{3,2,1,0:T(8,128)(2,1)} async-done(((bf16[4,2,128,768]{3,2,1,0:T(8,128)(2,1)}), bf16[4,2,128,768]{3,2,1,0:T(8,128)(2,1)}, u32[]{:S(2)}, u32[]{:S(2)}) %all-to-all-start.2) | async-done | bytes 1572896 | tf_op jit(solution)/shard_map/all_to_all | solution.py:153
  180.5 12.2 %fusion.7 = (bf16[4,2,128,2048]{3,2,0,1:T(8,128)(2,1)}, bf16[4,2,128,2048]{3,2,0,1:T(8,128)(2,1)S(1)}) fusion(f32[2,4,128,2048]{3,2,1,0:T(8,128)} %get-tuple-element.123, f32[2,4,128,2048]{3,2,1,0:T(8,128)} %copy-done.72, bf16[1,2,2048,768]{3,2,1,0:T(8,128)(2,1)} %param.35, bf16[4,2,128,768]{3,2,1,0:T(8,128)(2,1)} %all-to-all-done.2), kind=kOutput, calls=%fused_computation.22 | convolution fusion | flops 3252682752 | bytes 33030144 | tf_op jit(solution)/shard_map/secd,efd->secf/dot_general | solution.py:128
  192.8 7.1 %fusion.15 = f32[2,4,128,768]{3,2,1,0:T(8,128)S(1)} fusion(bf16[4,2,128,2048]{3,2,0,1:T(8,128)(2,1)S(1)} %get-tuple-element.95, bf16[1,2,768,2048]{3,2,1,0:T(8,128)(2,1)} %param.33), kind=kOutput, calls=%fused_computation.34 | convolution fusion | flops 3221225472 | bytes 13631488 | tf_op jit(solution)/shard_map/secf,edf->secd/dot_general | solution.py:136
  199.9 6.3 %fusion.57 = bf16[4,2,128,768]{3,2,0,1:T(8,128)(2,1)S(1)} fusion(f32[2,4,128,768]{3,2,1,0:T(8,128)S(1)} %fusion.15, bf16[4,2,128,2048]{3,2,0,1:T(8,128)(2,1)S(1)} %copy-done.11, bf16[1,2,768,2048]{3,2,1,0:T(8,128)(2,1)} %param.34), kind=kOutput, calls=%fused_computation.68 | convolution fusion | flops 3222798336 | bytes 15204352 | tf_op jit(solution)/shard_map/secf,edf->secd/dot_general | solution.py:137
  207.5 4.6 %all-to-all-start.4 = ((bf16[4,2,128,768]{3,2,1,0:T(8,128)(2,1)}), bf16[4,2,128,768]{3,2,1,0:T(8,128)(2,1)}, u32[]{:S(2)}, u32[]{:S(2)}) async-start(bf16[4,2,128,768]{3,2,1,0:T(8,128)(2,1)} %copy.190), calls=%async_computation.4 | async-start | bytes 3145728 | tf_op jit(solution)/shard_map/all_to_all | solution.py:153
  212.0 9.0 %convolution_bitcast_fusion = f32[1,2,768,2048]{3,2,1,0:T(8,128)} fusion(bf16[4,2,128,768]{3,2,1,0:T(8,128)(2,1)S(1)} %all-to-all-done.3, bf16[4,2,128,2048]{3,2,0,1:T(8,128)(2,1)} %get-tuple-element.94), kind=kOutput, calls=%fused_computation.52 | convolution fusion | flops 3221225472 | bytes 18350080 | tf_op jit(solution)/shard_map/secd,secf->edf/dot_general | solution.py:135
  221.0 8.1 %convolution_bitcast_fusion.2 = f32[1,2,2048,768]{3,2,1,0:T(8,128)} fusion(bf16[4,2,128,2048]{3,2,0,1:T(8,128)(2,1)S(1)} %copy-done.10, bf16[4,2,128,768]{3,2,1,0:T(8,128)(2,1)} %all-to-all-done.2), kind=kOutput, calls=%fused_computation.54 | convolution fusion | flops 3221225472 | bytes 18350080 | tf_op jit(solution)/shard_map/secf,secd->efd/dot_general | solution.py:129
  229.1 2.7 all-to-all-done.4
  231.8 3.9 gather_fusion.3
  235.7 2.3 reshape.1001
  238.0 2.3 select_reduce_fusion
  244.1 1.6 multiply_reduce_fusion.3
  247.5 5.2 %gather_fusion.5 = bf16[1024,768]{1,0:T(8,128)(2,1)} fusion(bf16[128,768]{1,0:T(8,128)(2,1)S(1)} %get-tuple-element.97, s32[1024]{0:T(1024)S(1)} %copy-done.51), kind=kCustom, calls=%fused_computation.clone | custom fusion | bytes 3149824 | tf_op jit(solution)/shard_map/jit(_take)/gather | solution.py:97
  252.8 2.9 select_select_fusion.1
  255.7 4.4 %all-to-all-start = ((bf16[4,2,128,768]{3,2,1,0:T(8,128)(2,1)}), bf16[4,2,128,768]{3,2,1,0:T(8,128)(2,1)}, u32[]{:S(2)}, u32[]{:S(2)}) async-start(bf16[4,2,128,768]{3,2,1,0:T(8,128)(2,1)} %bitcast.477), calls=%async_computation | async-start | bytes 3145728 | tf_op jit(solution)/shard_map/all_to_all | solution.py:153
  264.7 2.0 convolution_bitcast_fusion.4
  266.6 1.9 convolution_bitcast_fusion.3
  269.7 12.0 %all-to-all-done = bf16[4,2,128,768]{3,2,1,0:T(8,128)(2,1)} async-done(((bf16[4,2,128,768]{3,2,1,0:T(8,128)(2,1)}), bf16[4,2,128,768]{3,2,1,0:T(8,128)(2,1)}, u32[]{:S(2)}, u32[]{:S(2)}) %all-to-all-start) | async-done | bytes 1572896 | tf_op jit(solution)/shard_map/all_to_all | solution.py:153
  281.7 10.1 %fusion.25 = f32[2,4,128,2048]{3,2,1,0:T(8,128)} fusion(bf16[1,2,768,2048]{3,2,1,0:T(8,128)(2,1)} %param.34, bf16[4,2,128,768]{3,2,1,0:T(8,128)(2,1)} %all-to-all-done), kind=kOutput, calls=%fused_computation.44 | convolution fusion | flops 3221225472 | bytes 16252928 | tf_op jit(solution)/shard_map/secd,edf->secf/dot_general | solution.py:100
  291.8 9.9 %fusion.19 = f32[2,4,128,2048]{3,2,1,0:T(8,128)} fusion(bf16[1,2,768,2048]{3,2,1,0:T(8,128)(2,1)} %param.33, bf16[4,2,128,768]{3,2,1,0:T(8,128)(2,1)} %all-to-all-done), kind=kOutput, calls=%fused_computation.38 | convolution fusion | flops 3221225472 | bytes 16252928 | tf_op jit(solution)/shard_map/secd,edf->secf/dot_general | solution.py:99
  301.7 11.0 %fusion.52 = bf16[4,2,128,768]{3,2,0,1:T(8,128)(2,1)S(1)} fusion(bf16[1,2,2048,768]{3,2,1,0:T(8,128)(2,1)} %param.35, f32[2,4,128,2048]{3,2,1,0:T(8,128)} %fusion.25, f32[2,4,128,2048]{3,2,1,0:T(8,128)} %fusion.19), kind=kOutput, calls=%fused_computation.67 | convolution fusion | flops 3234594816 | bytes 24641536 | tf_op jit(solution)/shard_map/secf,efd->secd/dot_general | solution.py:102
  314.0 4.3 %all-to-all-start.1 = ((bf16[4,2,128,768]{3,2,1,0:T(8,128)(2,1)}), bf16[4,2,128,768]{3,2,1,0:T(8,128)(2,1)}, u32[]{:S(2)}, u32[]{:S(2)}) async-start(bf16[4,2,128,768]{3,2,1,0:T(8,128)(2,1)} %copy.179), calls=%async_computation.1 | async-start | bytes 3145728 | tf_op jit(solution)/shard_map/all_to_all | solution.py:153
  319.6 1.4 copy.176
  324.9 5.6 %collective-permute-start.1 = (bf16[1,128,768]{2,1,0:T(8,128)(2,1)}, bf16[1,128,768]{2,1,0:T(8,128)(2,1)S(1)}, u32[]{:S(2)}, u32[]{:S(2)}) collective-permute-start(bf16[1,128,768]{2,1,0:T(8,128)(2,1)} %fusion.136), channel_id=1, source_target_pairs={{0,12},{4,0},{8,4},{12,8},{1,13},{5,1},{9,5},{13,9},{2,14},{6,2},{... | collective-permute-start | bytes 589832 | tf_op jit(solution)/shard_map/ppermute | solution.py:168
  330.5 13.8 %all-to-all-done.1 = bf16[4,2,128,768]{3,2,1,0:T(8,128)(2,1)} async-done(((bf16[4,2,128,768]{3,2,1,0:T(8,128)(2,1)}), bf16[4,2,128,768]{3,2,1,0:T(8,128)(2,1)}, u32[]{:S(2)}, u32[]{:S(2)}) %all-to-all-start.1) | async-done | bytes 1572896 | tf_op jit(solution)/shard_map/all_to_all | solution.py:153
  344.4 3.9 gather_fusion
  348.3 2.3 reshape.998
  350.5 2.2 multiply_reduce_fusion.1
  352.8 3.2 collective-permute-start
  356.0 8.8 %convolution_bitcast_fusion.1 = f32[1,2,768,2048]{3,2,1,0:T(8,128)} fusion(bf16[4,2,128,768]{3,2,1,0:T(8,128)(2,1)S(1)} %all-to-all-done.3, bf16[4,2,128,2048]{3,2,0,1:T(8,128)(2,1)} %copy-done.8), kind=kOutput, calls=%fused_computation.53 | convolution fusion | flops 3221225472 | bytes 18350080 | tf_op jit(solution)/shard_map/secd,secf->edf/dot_general | solution.py:134
  364.8 12.3 %all-reduce = (f32[1,768]{1,0:T(1,128)}, f32[1,768]{1,0:T(1,128)}, f32[1,768,8]{1,2,0:T(8,128)}) all-reduce(f32[1,768]{1,0:T(1,128)S(1)} %broadcast_in_dim.223, f32[1,768]{1,0:T(1,128)S(1)} %broadcast_in_dim.224, f32[1,768,8]{1,2,0:T(8,128)S(1)} %copy-done.31), channel_id=1, replica_groups=mesh['dp'=2,'pp'=4,'ep'=4] {'ep'}, use_global_device_ids=true, to_apply=%region_33.35 | all-reduce | flops 7680 | bytes 61440 | tf_op jit(solution)/shard_map/psum | solution.py:166
  377.1 8.9 %all-reduce.4.cloned.1.call-done = (f32[1,768,6,128]{3,1,2,0:T(8,128)}, f32[1,768,1,128]{3,1,2,0:T(8,128)}, f32[1,768,1,128]{3,1,2,0:T(8,128)}, f32[1,6,128,768]{3,2,1,0:T(8,128)}) async-done(((f32[1,768,6,128]{3,1,2,0:T(8,128)}, f32[1,768,1,128]{3,1,2,0:T(8,128)}, f32[1,768,1,128]{3,1,2,0:T(8,128)}, f32[1,6,128,768]{3,2,1,0:T(8,128)}), (f32[1,768,6,128]{3,1,2,0:T(8,128)}, f32[1,768,1,128]{3,1,2,0:T(8,128)}, ...) | async-done | bytes 5505040 | tf_op jit(solution)/shard_map/psum | solution.py:166
  386.6 1.6 copy.264
  388.3 3.4 copy.265
  393.1 1.4 copy.268
  (254 shorter events, 66.5 us)
Async XLA Ops:
  7.2 24.8 %copy-start = (bf16[1,768,6,128]{3,1,2,0:T(8,128)(2,1)S(1)}, bf16[1,768,6,128]{3,1,2,0:T(8,128)(2,1)}, u32[]{:S(2)}) copy-start(bf16[1,768,6,128]{3,1,2,0:T(8,128)(2,1)} %param.28) | copy-start | bytes 3538948
  7.2 26.2 %copy-start.21 = (bf16[1,1,128,768]{3,2,1,0:T(8,128)(2,1)S(1)}, bf16[1,1,128,768]{3,2,1,0:T(8,128)(2,1)}, u32[]{:S(2)}) copy-start(bf16[1,1,128,768]{3,2,1,0:T(8,128)(2,1)} %param.19) | copy-start | bytes 589828
  7.2 26.8 %copy-start.27 = (pred[128,128]{0,1:T(8,128)(4,1)}, pred[128,128]{0,1:T(8,128)(4,1)S(1)}, u32[]{:S(2)}) copy-start(pred[128,128]{0,1:T(8,128)(4,1)S(1)} %iota_compare_fusion) | copy-start | bytes 49156
  9.5 24.5 %copy-start.42 = (f32[128]{0:T(128)}, f32[128]{0:T(128)S(1)}, u32[]{:S(2)}) copy-start(f32[128]{0:T(128)S(1)} %add_rsqrt_fusion.1) | copy-start | bytes 1540
  19.0 24.8 %copy-start.32 = (f32[768]{0:T(1024)}, f32[768]{0:T(1024)S(1)}, u32[]{:S(2)}) copy-start(f32[768]{0:T(1024)S(1)} %convert_reduce_fusion) | copy-start | bytes 9220
  31.4 13.0 %copy-start.39 = (s32[1024]{0:T(1024)}, s32[1024]{0:T(1024)S(1)}, u32[]{:S(2)}) copy-start(s32[1024]{0:T(1024)S(1)} %get-tuple-element.99) | copy-start | bytes 12292
  32.0 6.7 %copy-start.1 = (bf16[1,1,128,768]{3,2,1,0:T(8,128)(2,1)S(1)}, bf16[1,1,128,768]{3,2,1,0:T(8,128)(2,1)}, u32[]{:S(2)}) copy-start(bf16[1,1,128,768]{3,2,1,0:T(8,128)(2,1)} %param.20) | copy-start | bytes 589828
  32.0 6.7 %copy-start.6 = (bf16[1,6,128,768]{3,2,1,0:T(8,128)(2,1)S(1)}, bf16[1,6,128,768]{3,2,1,0:T(8,128)(2,1)}, u32[]{:S(2)}) copy-start(bf16[1,6,128,768]{3,2,1,0:T(8,128)(2,1)} %param.31) | copy-start | bytes 3538948
  33.4 6.3 %copy-start.15 = (bf16[128,6,128]{2,0,1:T(8,128)(2,1)}, bf16[128,6,128]{2,0,1:T(8,128)(2,1)S(1)}, u32[]{:S(2)}) copy-start(bf16[128,6,128]{2,0,1:T(8,128)(2,1)S(1)} %fusion.82) | copy-start | bytes 589828
  39.7 9.9 %copy-start.2 = (f32[128,768]{1,0:T(8,128)}, f32[128,768]{1,0:T(8,128)S(1)}, u32[]{:S(2)}) copy-start(f32[128,768]{1,0:T(8,128)S(1)} %get-tuple-element.121) | copy-start | bytes 1179652
  44.4 5.2 %copy-start.55 = (pred[1024]{0:T(1024)(128)(4,1)S(1)}, pred[1024]{0:T(1024)(128)(4,1)}, u32[]{:S(2)}) copy-start(pred[1024]{0:T(1024)(128)(4,1)} %get-tuple-element.131) | copy-start | bytes 3076
  49.6 7.7 %copy-start.66 = (s32[1,1,128,2]{2,3,1,0:T(2,128)S(1)}, s32[1,1,128,2]{2,3,1,0:T(2,128)}, u32[]{:S(2)}) copy-start(s32[1,1,128,2]{2,3,1,0:T(2,128)} %param.22) | copy-start | bytes 3076
  49.6 9.2 %copy-start.30 = (bf16[1,768,8]{1,2,0:T(8,128)(2,1)S(1)}, bf16[1,768,8]{1,2,0:T(8,128)(2,1)}, u32[]{:S(2)}) copy-start(bf16[1,768,8]{1,2,0:T(8,128)(2,1)} %param.32) | copy-start | bytes 36868
  52.5 24.6 %all-to-all-start.3 = ((bf16[4,2,128,768]{3,2,1,0:T(8,128)(2,1)}), bf16[4,2,128,768]{3,2,1,0:T(8,128)(2,1)S(1)}, u32[]{:S(2)}, u32[]{:S(2)}) async-start(bf16[4,2,128,768]{3,2,1,0:T(8,128)(2,1)} %bitcast.478), calls=%async_computation.3 | async-start | bytes 3145728 | tf_op jit(solution)/shard_map/all_to_all | solution.py:153
  77.1 18.0 %slice-start = ((s8[6291456]{0:T(1024)(128)(4,1)}), s8[4194304]{0:T(1024)(128)(4,1)S(1)}, s32[]{:S(2)}) async-start(s8[6291456]{0:T(1024)(128)(4,1)} %bitcast.499), calls=%async_computation.7 | async-start | bytes 8388608
  82.8 12.3 %copy-start.72 = (f32[2,4,128,2048]{3,2,1,0:T(8,128)}, f32[2,4,128,2048]{3,2,1,0:T(8,128)S(1)}, u32[]{:S(2)}) copy-start(f32[2,4,128,2048]{3,2,1,0:T(8,128)S(1)} %fusion.23) | copy-start | bytes 25165828
  82.8 12.3 %slice-start.1 = ((s8[6291456]{0:T(1024)(128)(4,1)}), s8[2097152]{0:T(1024)(128)(4,1)S(1)}, s32[]{:S(2)}) async-start(s8[6291456]{0:T(1024)(128)(4,1)} %bitcast.499), calls=%async_computation.8 | async-start | bytes 4194304
  99.8 35.1 %all-to-all-start.5 = ((bf16[4,2,128,768]{3,2,1,0:T(8,128)(2,1)}), bf16[4,2,128,768]{3,2,1,0:T(8,128)(2,1)}, u32[]{:S(2)}, u32[]{:S(2)}) async-start(bf16[4,2,128,768]{3,2,1,0:T(8,128)(2,1)} %copy.191), calls=%async_computation.5 | async-start | bytes 3145728 | tf_op jit(solution)/shard_map/all_to_all | solution.py:153
  143.4 9.5 %copy-start.35 = (s32[1024]{0:T(1024)S(1)}, s32[1024]{0:T(1024)}, u32[]{:S(2)}) copy-start(s32[1024]{0:T(1024)} %copy-done.34) | copy-start | bytes 12292
  143.4 9.5 %copy-start.56 = (pred[1024]{0:T(1024)(128)(4,1)S(1)}, pred[1024]{0:T(1024)(128)(4,1)}, u32[]{:S(2)}) copy-start(pred[1024]{0:T(1024)(128)(4,1)} %get-tuple-element.131) | copy-start | bytes 3076
  143.4 9.5 %copy-start.59 = (pred[4,2,128]{2,1,0:T(4,128)(4,1)S(1)}, pred[4,2,128]{2,1,0:T(4,128)(4,1)}, u32[]{:S(2)}) copy-start(pred[4,2,128]{2,1,0:T(4,128)(4,1)} %broadcast_in_dim.210) | copy-start | bytes 3076
  152.9 7.8 %copy-start.53 = (s32[256,1]{0,1:T(1,128)S(1)}, s32[256,1]{0,1:T(1,128)}, u32[]{:S(2)}) copy-start(s32[256,1]{0,1:T(1,128)} %reshape_squeeze.4) | copy-start | bytes 3076
  152.9 7.8 %copy-start.58 = (s32[256]{0:T(256)S(1)}, s32[256]{0:T(256)}, u32[]{:S(2)}) copy-start(s32[256]{0:T(256)} %copy-done.57) | copy-start | bytes 3076
  152.9 7.8 %copy-start.68 = (s32[256]{0:T(256)S(1)}, s32[256]{0:T(256)}, u32[]{:S(2)}) copy-start(s32[256]{0:T(256)} %get-tuple-element.91) | copy-start | bytes 3076
  152.9 11.0 %copy-start.69 = (pred[256]{0:T(512)(128)(4,1)S(1)}, pred[256]{0:T(512)(128)(4,1)}, u32[]{:S(2)}) copy-start(pred[256]{0:T(512)(128)(4,1)} %get-tuple-element.90) | copy-start | bytes 772
  152.9 13.6 %copy-start.62 = (pred[128,2]{0,1:T(4,128)(4,1)S(1)}, pred[128,2]{0,1:T(4,128)(4,1)}, u32[]{:S(2)}) copy-start(pred[128,2]{0,1:T(4,128)(4,1)} %copy.192) | copy-start | bytes 772
  153.0 13.6 %copy-start.54 = (s32[1,1,128,2]{2,3,1,0:T(2,128)S(1)}, s32[1,1,128,2]{2,3,1,0:T(2,128)}, u32[]{:S(2)}) copy-start(s32[1,1,128,2]{2,3,1,0:T(2,128)} %param.23) | copy-start | bytes 3076
  156.4 24.2 %all-to-all-start.2 = ((bf16[4,2,128,768]{3,2,1,0:T(8,128)(2,1)}), bf16[4,2,128,768]{3,2,1,0:T(8,128)(2,1)}, u32[]{:S(2)}, u32[]{:S(2)}) async-start(bf16[4,2,128,768]{3,2,1,0:T(8,128)(2,1)} %multiply_convert_fusion), calls=%async_computation.2 | async-start | bytes 3145728 | tf_op jit(solution)/shard_map/all_to_all | solution.py:153
  166.6 26.2 %copy-start.40 = (bf16[128,8]{0,1:T(8,128)(2,1)}, bf16[128,8]{0,1:T(8,128)(2,1)S(1)}, u32[]{:S(2)}) copy-start(bf16[128,8]{0,1:T(8,128)(2,1)S(1)} %select_reduce_fusion.1) | copy-start | bytes 6148
  192.7 7.2 %copy-start.8 = (bf16[4,2,128,2048]{3,2,0,1:T(8,128)(2,1)}, bf16[4,2,128,2048]{3,2,0,1:T(8,128)(2,1)S(1)}, u32[]{:S(2)}) copy-start(bf16[4,2,128,2048]{3,2,0,1:T(8,128)(2,1)S(1)} %get-tuple-element.95) | copy-start | bytes 12582916
  192.7 7.2 %copy-start.11 = (bf16[4,2,128,2048]{3,2,0,1:T(8,128)(2,1)S(1)}, bf16[4,2,128,2048]{3,2,0,1:T(8,128)(2,1)}, u32[]{:S(2)}) copy-start(bf16[4,2,128,2048]{3,2,0,1:T(8,128)(2,1)} %get-tuple-element.94) | copy-start | bytes 12582916
  207.5 24.3 %all-to-all-start.4 = ((bf16[4,2,128,768]{3,2,1,0:T(8,128)(2,1)}), bf16[4,2,128,768]{3,2,1,0:T(8,128)(2,1)}, u32[]{:S(2)}, u32[]{:S(2)}) async-start(bf16[4,2,128,768]{3,2,1,0:T(8,128)(2,1)} %copy.190), calls=%async_computation.4 | async-start | bytes 3145728 | tf_op jit(solution)/shard_map/all_to_all | solution.py:153
  212.0 9.0 %copy-start.10 = (bf16[4,2,128,2048]{3,2,0,1:T(8,128)(2,1)S(1)}, bf16[4,2,128,2048]{3,2,0,1:T(8,128)(2,1)}, u32[]{:S(2)}) copy-start(bf16[4,2,128,2048]{3,2,0,1:T(8,128)(2,1)} %copy-done.9) | copy-start | bytes 12582916
  229.1 8.9 %copy-start.28 = (pred[128,2]{1,0:T(8,128)(4,1)S(1)}, pred[128,2]{1,0:T(8,128)(4,1)}, u32[]{:S(2)}) copy-start(pred[128,2]{1,0:T(8,128)(4,1)} %lt.117) | copy-start | bytes 772
  229.1 11.2 %copy-start.3 = (f32[128,768]{1,0:T(8,128)S(1)}, f32[128,768]{1,0:T(8,128)}, u32[]{:S(2)}) copy-start(f32[128,768]{1,0:T(8,128)} %copy-done.2) | copy-start | bytes 1179652
  229.1 11.2 %copy-start.33 = (f32[768]{0:T(1024)S(1)}, f32[768]{0:T(1024)}, u32[]{:S(2)}) copy-start(f32[768]{0:T(1024)} %copy-done.32) | copy-start | bytes 9220
  229.1 11.3 %copy-start.41 = (bf16[128,8]{0,1:T(8,128)(2,1)S(1)}, bf16[128,8]{0,1:T(8,128)(2,1)}, u32[]{:S(2)}) copy-start(bf16[128,8]{0,1:T(8,128)(2,1)} %copy-done.40) | copy-start | bytes 6148
  229.1 11.3 %copy-start.61 = (f32[128]{0:T(128)S(1)}, f32[128]{0:T(128)}, u32[]{:S(2)}) copy-start(f32[128]{0:T(128)} %copy-done.60) | copy-start | bytes 1540
  237.9 5.3 %copy-start.7 = (bf16[1,6,128,768]{3,2,1,0:T(8,128)(2,1)S(1)}, bf16[1,6,128,768]{3,2,1,0:T(8,128)(2,1)}, u32[]{:S(2)}) copy-start(bf16[1,6,128,768]{3,2,1,0:T(8,128)(2,1)} %param.31) | copy-start | bytes 3538948
  238.0 5.8 %copy-start.13 = (f32[1,1,6,128,128]{3,4,2,1,0:T(8,128)S(1)}, f32[1,1,6,128,128]{3,4,2,1,0:T(8,128)}, u32[]{:S(2)}) copy-start(f32[1,1,6,128,128]{3,4,2,1,0:T(8,128)} %copy-done.12) | copy-start | bytes 1179652
  238.0 5.8 %copy-start.37 = (f32[6,128]{1,0:T(8,128)S(1)}, f32[6,128]{1,0:T(8,128)}, u32[]{:S(2)}) copy-start(f32[6,128]{1,0:T(8,128)} %copy-done.36) | copy-start | bytes 9220
  238.0 5.9 %copy-start.46 = (f32[6,128]{1,0:T(8,128)S(1)}, f32[6,128]{1,0:T(8,128)}, u32[]{:S(2)}) copy-start(f32[6,128]{1,0:T(8,128)} %copy-done.45) | copy-start | bytes 9220
  244.1 8.6 %copy-start.29 = (bf16[128,128]{0,1:T(8,128)(2,1)}, bf16[128,128]{0,1:T(8,128)(2,1)S(1)}, u32[]{:S(2)}) copy-start(bf16[128,128]{0,1:T(8,128)(2,1)S(1)} %fusion.113) | copy-start | bytes 98308
  245.9 6.9 %copy-start.49 = (f32[128,2]{0,1:T(2,128)}, f32[128,2]{0,1:T(2,128)S(1)}, u32[]{:S(2)}) copy-start(f32[128,2]{0,1:T(2,128)S(1)} %select_reduce_fusion.3) | copy-start | bytes 3076
  247.5 5.2 %copy-start.64 = (pred[1024]{0:T(1024)(128)(4,1)S(1)}, pred[1024]{0:T(1024)(128)(4,1)}, u32[]{:S(2)}) copy-start(pred[1024]{0:T(1024)(128)(4,1)} %get-tuple-element.134) | copy-start | bytes 3076
  247.5 5.2 %copy-start.65 = (pred[1024]{0:T(1024)(128)(4,1)S(1)}, pred[1024]{0:T(1024)(128)(4,1)}, u32[]{:S(2)}) copy-start(pred[1024]{0:T(1024)(128)(4,1)} %get-tuple-element.135) | copy-start | bytes 3076
  252.8 7.6 %copy-start.38 = (f32[6,128]{1,0:T(8,128)S(1)}, f32[6,128]{1,0:T(8,128)}, u32[]{:S(2)}) copy-start(f32[6,128]{1,0:T(8,128)} %copy-done.36) | copy-start | bytes 9220
  252.8 7.6 %copy-start.47 = (f32[6,128]{1,0:T(8,128)S(1)}, f32[6,128]{1,0:T(8,128)}, u32[]{:S(2)}) copy-start(f32[6,128]{1,0:T(8,128)} %copy-done.45) | copy-start | bytes 9220
  252.8 8.9 %copy-start.16 = (bf16[128,6,128]{2,0,1:T(8,128)(2,1)S(1)}, bf16[128,6,128]{2,0,1:T(8,128)(2,1)}, u32[]{:S(2)}) copy-start(bf16[128,6,128]{2,0,1:T(8,128)(2,1)} %copy-done.15) | copy-start | bytes 589828
  252.8 9.8 %copy-start.44 = (f32[128]{0:T(128)S(1)}, f32[128]{0:T(128)}, u32[]{:S(2)}) copy-start(f32[128]{0:T(128)} %copy-done.42) | copy-start | bytes 1540
  255.7 26.0 %all-to-all-start = ((bf16[4,2,128,768]{3,2,1,0:T(8,128)(2,1)}), bf16[4,2,128,768]{3,2,1,0:T(8,128)(2,1)}, u32[]{:S(2)}, u32[]{:S(2)}) async-start(bf16[4,2,128,768]{3,2,1,0:T(8,128)(2,1)} %bitcast.477), calls=%async_computation | async-start | bytes 3145728 | tf_op jit(solution)/shard_map/all_to_all | solution.py:153
  260.1 6.6 %copy-start.5 = (f32[128,768]{1,0:T(8,128)S(1)}, f32[128,768]{1,0:T(8,128)}, u32[]{:S(2)}) copy-start(f32[128,768]{1,0:T(8,128)} %copy-done.4) | copy-start | bytes 1179652
  260.1 125.9 %all-reduce.4.cloned.1.call-start = ((), (), s32[]{:S(2)}) async-start(), calls=%async_computation.6 | async-start | bytes 11010048 | tf_op jit(solution)/shard_map/psum | solution.py:166
  260.4 6.3 %copy-start.20 = (bf16[128,6,128]{0,2,1:T(8,128)(2,1)S(1)}, bf16[128,6,128]{0,2,1:T(8,128)(2,1)}, u32[]{:S(2)}) copy-start(bf16[128,6,128]{0,2,1:T(8,128)(2,1)} %copy-done.19) | copy-start | bytes 589828
  314.0 30.4 %all-to-all-start.1 = ((bf16[4,2,128,768]{3,2,1,0:T(8,128)(2,1)}), bf16[4,2,128,768]{3,2,1,0:T(8,128)(2,1)}, u32[]{:S(2)}, u32[]{:S(2)}) async-start(bf16[4,2,128,768]{3,2,1,0:T(8,128)(2,1)} %copy.179), calls=%async_computation.1 | async-start | bytes 3145728 | tf_op jit(solution)/shard_map/all_to_all | solution.py:153
  324.0 26.5 %copy-start.25 = (f32[128,2]{1,0:T(8,128)S(1)}, f32[128,2]{1,0:T(8,128)}, u32[]{:S(2)}) copy-start(f32[128,2]{1,0:T(8,128)} %copy.176) | copy-start | bytes 3076
  324.9 27.8 %copy-start.17 = (f32[128,768]{1,0:T(8,128)S(1)}, f32[128,768]{1,0:T(8,128)}, u32[]{:S(2)}) copy-start(f32[128,768]{1,0:T(8,128)} %get-tuple-element.126) | copy-start | bytes 1179652
  324.9 52.2 %collective-permute-start.1 = (bf16[1,128,768]{2,1,0:T(8,128)(2,1)}, bf16[1,128,768]{2,1,0:T(8,128)(2,1)S(1)}, u32[]{:S(2)}, u32[]{:S(2)}) collective-permute-start(bf16[1,128,768]{2,1,0:T(8,128)(2,1)} %fusion.136), channel_id=1, source_target_pairs={{0,12},{4,0},{8,4},{12,8},{1,13},{5,1},{9,5},{13,9},{2,14},{6,2},{... | collective-permute-start | bytes 589832 | tf_op jit(solution)/shard_map/ppermute | solution.py:168
  352.7 12.0 %copy-start.48 = (f32[768]{0:T(1024)S(1)}, f32[768]{0:T(1024)}, u32[]{:S(2)}) copy-start(f32[768]{0:T(1024)} %get-tuple-element.73) | copy-start | bytes 9220
  352.7 12.0 %copy-start.31 = (f32[1,768,8]{1,2,0:T(8,128)S(1)}, f32[1,768,8]{1,2,0:T(8,128)}, u32[]{:S(2)}) copy-start(f32[1,768,8]{1,2,0:T(8,128)} %convolution_bitcast_fusion.13) | copy-start | bytes 73732
  352.8 24.3 %collective-permute-start = (bf16[1,128,768]{2,1,0:T(8,128)(2,1)S(1)}, bf16[1,128,768]{2,1,0:T(8,128)(2,1)S(1)}, u32[]{:S(2)}, u32[]{:S(2)}) collective-permute-start(bf16[1,128,768]{2,1,0:T(8,128)(2,1)S(1)} %fusion.134), channel_id=1, source_target_pairs={{0,4},{4,8},{8,12},{12,0},{1,5},{5,9},{9,13},{13,1},{2,6},{6,10},{... | collective-permute-start | bytes 589832 | tf_op jit(solution)/shard_map/ppermute | solution.py:167
  377.1 8.9 %copy-start.26 = (bf16[1,128,768]{2,1,0:T(8,128)(2,1)}, bf16[1,128,768]{2,1,0:T(8,128)(2,1)S(1)}, u32[]{:S(2)}) copy-start(bf16[1,128,768]{2,1,0:T(8,128)(2,1)S(1)} %collective-permute-done.1) | copy-start | bytes 589828
  386.0 5.7 %copy-start.23 = (f32[1,768,1,128]{3,1,2,0:T(8,128)S(1)}, f32[1,768,1,128]{3,1,2,0:T(8,128)}, u32[]{:S(2)}) copy-start(f32[1,768,1,128]{3,1,2,0:T(8,128)} %get-tuple-element.81) | copy-start | bytes 1179652
  386.0 6.4 %copy-start.22 = (f32[1,768,1,128]{3,1,2,0:T(8,128)S(1)}, f32[1,768,1,128]{3,1,2,0:T(8,128)}, u32[]{:S(2)}) copy-start(f32[1,768,1,128]{3,1,2,0:T(8,128)} %get-tuple-element.82) | copy-start | bytes 1179652
  (20 other events, 45.9 us)
Sparse Core Ops, SparseCore 0:
  268.6 117.2 all-reduce.3
where the time goes:
time: 409 us; the launch traced here: 402 us
  matrix products  134 us (33%)
  local copies, waits for them, and re-layouts  82.2 us (20%)
  waiting for transfers between devices  67.2 us (16%)
  other arithmetic  54.9 us (13%)
  starting transfers between devices  35.9 us (9%)
  between operations  15.6 us (4%)
  blocking collectives  12.3 us (3%)
    all_to_all x6, waiting for transfers between devices, exchange(): return lax.all_to_all(send_block, 'ep', 0, 0, tiled=True)  58.3 us
    all_to_all x6, starting transfers between devices, exchange(): return lax.all_to_all(send_block, 'ep', 0, 0, tiled=True)  26.8 us
    dot_general x2, matrix products, moe_forward(): jnp.einsum('secd,edf->secf', recv_buf, w_1, preferred_element_type=jnp.fl...  22.2 us
    dot_general x2, matrix products, moe_forward(): jnp.einsum('secd,edf->secf', recv_buf, w_3, preferred_element_type=jnp.fl...  15.8 us
    dot_general x2, matrix products, moe_forward(): jnp.einsum('secf,efd->secd', act_bf, w_2, preferred_element_type=jnp.floa...  14.5 us
    unnamed x158, local copies, waits for them, and re-layouts  14.1 us
    psum x1, blocking collectives, device_tick(): lax.psum((d_gain_1, d_gain_2, d_w_q, d_w_k, d_w_v, d_w_o, d_w_r), 'ep')  12.3 us
    dot_general x1, matrix products, moe_backward(): jnp.einsum('secd,efd->secf', d_expert, w_2, preferred_element_type=jnp.fl...  12.2 us
  transfers between devices with their start and end apart: 9, of which 6 were waited for; matrix products, arithmetic and copies ran while one was open for 30% of the time, Pallas kernels for 0%

commit v1 on v0

v1 whole, which is shorter than its diff:
```python
import functools

import jax
import jax.numpy as jnp
from jax import lax
from jax.experimental import pallas as pl
from jax.experimental.pallas import tpu as pltpu
from jax.sharding import PartitionSpec as P

NORM_EPS = 1e-6
MASK_VALUE = -1e30
F32 = jnp.float32
BF16 = jnp.bfloat16
MESH = pl.DeviceIdType.MESH
VMEM = pltpu.VMEM
FFN_TILE = 256
LANES = 128


def dot_nn(lhs, rhs):
    return lax.dot_general(lhs, rhs, (((1,), (0,)), ((), ())), preferred_element_type=F32)


def dot_nt(lhs, rhs):
    return lax.dot_general(lhs, rhs, (((1,), (1,)), ((), ())), preferred_element_type=F32)


def dot_tn(lhs, rhs):
    return lax.dot_general(lhs, rhs, (((0,), (0,)), ((), ())), preferred_element_type=F32)


def ep_peers():
    me = lax.axis_index('ep')
    partner = me + 1 - 2 * lax.rem(me, 2)
    across = lax.rem(me + 2, 4)
    diag = lax.rem(partner + 2, 4)
    return me, partner, across, diag


def greet(peers):
    barrier = pltpu.get_barrier_semaphore()
    for peer in peers:
        pl.semaphore_signal(barrier, inc=1, device_id=peer, device_id_type=MESH)
    pl.semaphore_wait(barrier, len(peers))


def push(src, dst, sems, idx, peer):
    return pltpu.make_async_remote_copy(src_ref=src, dst_ref=dst, send_sem=sems[0].at[idx], recv_sem=sems[1].at[idx],
                                        device_id=peer, device_id_type=MESH)


def stack_heads(wide, heads, head_dim):
    return jnp.concatenate([wide[:, h * head_dim:(h + 1) * head_dim] for h in range(heads)], axis=0)


def unstack_heads(tall, heads, seq_len):
    return jnp.concatenate([tall[h * seq_len:(h + 1) * seq_len] for h in range(heads)], axis=1)


def rms_inv(x_f32):
    return lax.rsqrt(jnp.mean(x_f32 * x_f32, axis=-1, keepdims=True) + NORM_EPS)


def attention_rows(x_bf, gain, wq, wk, wv, wo, n_seq, heads):
    seq_len, head_dim = x_bf.shape[0] // n_seq, wk.shape[1]
    x_f32 = x_bf.astype(F32)
    normed = (x_f32 * rms_inv(x_f32) * gain).astype(BF16)
    query = dot_nn(normed, wq).astype(BF16)
    key = dot_nn(normed, wk).astype(BF16)
    value = dot_nn(normed, wv).astype(BF16)
    row = lax.rem(lax.broadcasted_iota(jnp.int32, (heads * seq_len, seq_len), 0), seq_len)
    col = lax.broadcasted_iota(jnp.int32, (heads * seq_len, seq_len), 1)
    causal = row >= col
    outs, probs_all = [], []
    for s in range(n_seq):
        rows = slice(s * seq_len, (s + 1) * seq_len)
        scores = dot_nt(stack_heads(query[rows], heads, head_dim), key[rows]) * head_dim ** -0.5
        scores = jnp.where(causal, scores, MASK_VALUE)
        expd = jnp.exp(scores - jnp.max(scores, axis=-1, keepdims=True))
        probs = expd / jnp.sum(expd, axis=-1, keepdims=True)
        probs_all.append(probs)
        outs.append(unstack_heads(dot_nn(probs.astype(BF16), value[rows]).astype(BF16), heads, seq_len))
    attn = jnp.concatenate(outs, axis=0)
    hidden = (x_f32 + dot_nn(attn, wo)).astype(BF16)
    return hidden, (normed, query, key, value, probs_all, attn)


def route_rows(hidden, gain, wr, cols, counts, base, n_seq):
    seq_len = hidden.shape[0] // n_seq
    h_f32 = hidden.astype(F32)
    normed = (h_f32 * rms_inv(h_f32) * gain).astype(BF16)
    logits = dot_nn(normed, wr)
    lane = lax.broadcasted_iota(jnp.int32, (seq_len, LANES), 1).astype(F32)
    lower = (lax.broadcasted_iota(jnp.int32, (seq_len, seq_len), 0)
             > lax.broadcasted_iota(jnp.int32, (seq_len, seq_len), 1)).astype(F32).astype(BF16)
    weights, masks, routes = [], [], []
    for s in range(n_seq):
        id0, id1 = cols[s][base], cols[s][base + 1]
        hot0, hot1 = (lane == id0).astype(F32), (lane == id1).astype(F32)
        rank = dot_nn(lower, (hot0 + hot1).astype(BF16))
        rank1 = rank + (id0 == id1).astype(F32)
        kept0 = hot0 * (rank < counts[s]).astype(F32)
        kept1 = hot1 * (rank1 < counts[s]).astype(F32)
        part = logits[s * seq_len:(s + 1) * seq_len]
        sel0 = jnp.sum(jnp.where(hot0 > 0, part, 0.0), axis=-1, keepdims=True)
        sel1 = jnp.sum(jnp.where(hot1 > 0, part, 0.0), axis=-1, keepdims=True)
        top = jnp.maximum(sel0, sel1)
        exp0, exp1 = jnp.exp(sel0 - top), jnp.exp(sel1 - top)
        gate0, gate1 = exp0 / (exp0 + exp1), exp1 / (exp0 + exp1)
        weights.append(kept0 * gate0 + kept1 * gate1)
        masks.append(jnp.maximum(kept0, kept1))
        keep0 = jnp.sum(kept0, axis=-1, keepdims=True)
        keep1 = jnp.sum(kept1, axis=-1, keepdims=True)
        route = jnp.zeros((seq_len, LANES), F32)
        for i, item in enumerate((id0, id1, gate0, gate1, keep0, keep1)):
            route = jnp.where(lane == i, item, route)
        routes.append(route)
    return normed, jnp.concatenate(weights, 0), jnp.concatenate(masks, 0), jnp.concatenate(routes, 0)


def head_kernel(n_ep, heads, pk_ref, xa_ref, xb_ref, gb_ref, gain1_ref, gain2_ref, wq_ref, wk_ref, wv_ref, wo_ref, wr_ref,
                xb_all, gb_all, n2a_ref, n2b_ref, wta_ref, ma_ref, wtb_ref, mb_ref, rtb_ref, ha_ref, hb_ref,
                n1_ref, q_ref, k_ref, v_ref, p_ref, o_ref,
                xa_all, pk_all, wq_s, wr_s, send_sem, recv_sem):
    me, partner, across, diag = ep_peers()
    seq_len = xa_ref.shape[0]
    sems = (send_sem, recv_sem)
    greet(({'ep': partner}, {'ep': across}))
    own, landing = (pk_ref, xb_ref, xa_ref, gb_ref), (pk_all, xb_all, xa_all, gb_all)
    near, far, relay = [], [], []
    for i in range(4):
        far.append(push(own[i], landing[i].at[me], sems, 3 * i, {'ep': across}))
        far[i].start()
        near.append(push(own[i], landing[i].at[me], sems, 3 * i + 1, {'ep': partner}))
        near[i].start()
        relay.append(push(landing[i].at[across], landing[i].at[across], sems, 3 * i + 2, {'ep': partner}))
        landing[i][me] = own[i][...]

    def arrive(i):
        far[i].wait_recv()
        relay[i].start()
        near[i].wait_recv()
        relay[i].wait_recv()

    for h in range(heads):
        wq_s[:, h * LANES:(h + 1) * LANES] = wq_ref[h]
    wr_s[...] = jnp.zeros_like(wr_s)
    wr_s[0:wr_ref.shape[0], :] = wr_ref[...]
    wr = wr_s[...].T
    gain1, gain2 = gain1_ref[...].astype(F32), gain2_ref[...].astype(F32)

    arrive(0)
    packed = pk_all[...].astype(F32)
    flat = jnp.concatenate([packed[s] for s in range(n_ep)] + [jnp.zeros((LANES - 8 * n_ep, LANES), F32)], axis=0).T
    cols = [[flat[:, 8 * s + r:8 * s + r + 1] for r in range(4)] for s in range(n_ep)]
    counts_a = [packed[s, 4:5, :] for s in range(n_ep)]
    counts_b = [packed[s, 5:6, :] for s in range(n_ep)]

    def rows_of(ref):
        return jnp.concatenate([ref[s] for s in range(n_ep)], axis=0)

    arrive(1)
    hidden, (normed, query, key, value, probs, attn) = attention_rows(
        rows_of(xb_all), gain1, wq_s[...], wk_ref[...], wv_ref[...], wo_ref[...], n_ep, heads)
    n1_ref[...], q_ref[...], k_ref[...], v_ref[...], o_ref[...] = normed, query, key, value, attn
    for s in range(n_ep):
        p_ref[s] = probs[s]
    hb_ref[...] = hidden
    n2b_ref[...], wtb_ref[...], mb_ref[...], rtb_ref[...] = route_rows(hidden, gain2, wr, cols, counts_b, 2, n_ep)

    arrive(2)
    hidden, _ = attention_rows(rows_of(xa_all), gain1, wq_s[...], wk_ref[...], wv_ref[...], wo_ref[...], n_ep, heads)
    ha_ref[...] = hidden
    n2a_ref[...], wta_ref[...], ma_ref[...], _ = route_rows(hidden, gain2, wr, cols, counts_a, 0, n_ep)

    arrive(3)
    for i in range(4):
        far[i].wait_send()
        near[i].wait_send()
        relay[i].wait_send()


def moe_kernel(e_local, n2a_ref, n2b_ref, g_ref, wta_ref, ma_ref, wtb_ref, mb_ref, w1_ref, w3_ref, w2_ref,
               ra_ref, rb_ref, dw1_ref, dw3_ref, dw2_ref, xm, xbt, dexp, acc, dacc, col):
    expert, tile = pl.program_id(0), pl.program_id(1)
    n_tok, d_model = n2a_ref.shape
    here = lax.axis_index('ep') * e_local + expert

    @pl.when(tile == 0)
    def _():
        lane = lax.broadcasted_iota(jnp.int32, (n_tok, LANES), 1)
        mine = lane == here

        def column(ref):
            return jnp.sum(jnp.where(mine, ref[...], 0.0), axis=-1, keepdims=True)
        wt_a, m_a, wt_b, m_b = column(wta_ref), column(ma_ref), column(wtb_ref), column(mb_ref)
        for i, item in enumerate((wt_a, m_a, m_b)):
            col[i] = jnp.broadcast_to(item, (n_tok, LANES))
        xm[0:n_tok, :] = jnp.where(m_a > 0, n2a_ref[...].astype(F32), 0.0).astype(BF16)
        x_b = jnp.where(m_b > 0, n2b_ref[...].astype(F32), 0.0)
        xm[n_tok:, :] = x_b.astype(BF16)
        xbt[...] = x_b.T.astype(BF16)
        dexp[...] = jnp.where(m_b > 0, wt_b * g_ref[...].astype(F32), 0.0).astype(BF16)
        acc[...] = jnp.zeros_like(acc)
        dacc[...] = jnp.zeros_like(dacc)

    @pl.when((tile == 0) & (expert == 0))
    def _():
        ra_ref[...] = jnp.zeros_like(ra_ref)
        rb_ref[...] = jnp.zeros_like(rb_ref)

    w1, w3, w2 = w1_ref[0], w3_ref[0], w2_ref[0]
    x_all = xm[...]
    gate_pre, up_pre = dot_nn(x_all, w1), dot_nn(x_all, w3)
    sig = jax.nn.sigmoid(gate_pre)
    act = (gate_pre * sig * up_pre).astype(BF16)
    acc[...] += dot_nn(act, w2)
    gate_b, up_b, sig_b = gate_pre[n_tok:], up_pre[n_tok:], sig[n_tok:]
    d_exp = dexp[...]
    d_act = dot_nt(d_exp, w2).astype(BF16).astype(F32)
    d_up = (d_act * gate_b * sig_b).astype(BF16)
    d_gate = (d_act * up_b * sig_b * (1.0 + gate_b * (1.0 - sig_b))).astype(BF16)
    x_t = xbt[...]
    dw1_ref[0] = dot_nn(x_t, d_gate)
    dw3_ref[0] = dot_nn(x_t, d_up)
    dw2_ref[0] = dot_tn(act[n_tok:], d_exp)
    dacc[...] += dot_nt(d_gate, w1) + dot_nt(d_up, w3)

    @pl.when(tile == pl.num_programs(1) - 1)
    def _():
        out_a = acc[0:n_tok, :].astype(BF16).astype(F32)
        ra_ref[...] += jnp.where(col[1][:, 0:1] > 0, col[0][:, 0:1] * out_a, 0.0)
        out_b = acc[n_tok:, :].astype(BF16).astype(F32)
        in_b = col[2][:, 0:1] > 0
        rb_ref[:, 0:d_model] += jnp.where(in_b, dacc[...].astype(BF16).astype(F32), 0.0)
        pick = jnp.sum(jnp.where(in_b, out_b * g_ref[...].astype(F32), 0.0), axis=-1, keepdims=True)
        lane = lax.broadcasted_iota(jnp.int32, (n_tok, LANES), 1)
        rb_ref[:, d_model:] += jnp.where(lane == here, pick, 0.0)


def tail_kernel(n_ep, n_pp, heads, ra_ref, rb_ref, ha_ref, hb_ref, n2b_ref, gb_ref, rtb_ref, x_ref, n1_ref, q_ref, k_ref, v_ref,
                p_ref, o_ref, gain1_ref, gain2_ref, wq_ref, wk_ref, wv_ref, wo_ref, wr_ref,
                y_ref, dx_ref, dwq_ref, dwk_ref, dwv_ref, dwo_ref, dg1_ref, dg2_ref, dwr_ref,
                near_b, swap_b, sum_b, far_b, near_a, swap_a, sum_a, far_a, dh_all, small, small_1, small_2, small_3,
                y_own, dx_all, wq_s, wr_s, send_sem, recv_sem):
    me, partner, across, diag = ep_peers()
    stage = lax.axis_index('pp')
    later, earlier = lax.rem(stage + 1, n_pp), lax.rem(stage + n_pp - 1, n_pp)
    seq_len, d_model = y_ref.shape
    sems = (send_sem, recv_sem)
    near, over = {'ep': partner}, {'ep': across}
    greet((near, over, {'pp': later}, {'pp': earlier}))
    swap_b_c = push(rb_ref.at[diag], swap_b, sems, 0, near)
    near_b_c = push(rb_ref.at[partner], near_b, sems, 1, near)
    swap_a_c = push(ra_ref.at[diag], swap_a, sems, 2, near)
    near_a_c = push(ra_ref.at[partner], near_a, sems, 3, near)
    far_b_c = push(sum_b, far_b, sems, 4, over)
    far_a_c = push(sum_a, far_a, sems, 5, over)
    swap_b_c.start()
    near_b_c.start()
    swap_a_c.start()
    near_a_c.start()
    for h in range(heads):
        wq_s[:, h * LANES:(h + 1) * LANES] = wq_ref[h]
    wr_s[...] = jnp.zeros_like(wr_s)
    wr_s[0:wr_ref.shape[0], :] = wr_ref[...]
    swap_b_c.wait_recv()
    sum_b[...] = rb_ref[across] + swap_b[...]
    far_b_c.start()
    swap_a_c.wait_recv()
    sum_a[...] = ra_ref[across] + swap_a[...]

    gain1, gain2 = gain1_ref[...].astype(F32), gain2_ref[...].astype(F32)
    mine = pl.ds(pl.multiple_of(me * seq_len, seq_len), seq_len)
    route = rtb_ref[mine, :]
    id0, id1, gate0, gate1, keep0, keep1 = [route[:, i:i + 1] for i in range(6)]
    lane = lax.broadcasted_iota(jnp.int32, (seq_len, LANES), 1).astype(F32)
    hot0, hot1 = (lane == id0).astype(F32), (lane == id1).astype(F32)
    h_f32 = hb_ref[mine, :].astype(F32)
    inv = rms_inv(h_f32)
    h_hat = h_f32 * inv
    near_b_c.wait_recv()
    far_b_c.wait_recv()
    total = rb_ref[me] + near_b[...] + far_b[...]
    dots = total[:, d_model:]
    d_gate0 = jnp.where(keep0 > 0, jnp.sum(hot0 * dots, axis=-1, keepdims=True), 0.0)
    d_gate1 = jnp.where(keep1 > 0, jnp.sum(hot1 * dots, axis=-1, keepdims=True), 0.0)
    mean_gate = gate0 * d_gate0 + gate1 * d_gate1
    d_logits = (hot0 * (gate0 * (d_gate0 - mean_gate)) + hot1 * (gate1 * (d_gate1 - mean_gate))).astype(BF16)
    d_normed = total[:, :d_model] + dot_nn(d_logits, wr_s[...])
    d_hat = d_normed * gain2
    d_in = inv * (d_hat - h_hat * jnp.mean(d_hat * h_hat, axis=-1, keepdims=True))
    dh_all[me] = (d_in + gb_ref[me].astype(F32)).astype(BF16)
    dh_far = push(dh_all.at[me], dh_all.at[me], sems, 6, over)
    dh_near = push(dh_all.at[me], dh_all.at[me], sems, 7, near)
    dh_relay = push(dh_all.at[across], dh_all.at[across], sems, 8, near)
    dh_far.start()
    dh_near.start()
    small[0:8, :] = dot_tn(d_logits, n2b_ref[mine, :])[0:8, :]
    small[8:16, :] = jnp.broadcast_to(jnp.sum(d_normed * h_hat, axis=0, keepdims=True), (8, d_model))
    small_near = push(small, small_1, sems, 9, near)
    small_near.start()
    small_near.wait_recv()
    small_2[...] = small[...] + small_1[...]
    small_far = push(small_2, small_3, sems, 10, over)
    small_far.start()
    far_a_c.start()
    dh_far.wait_recv()
    dh_relay.start()
    dh_near.wait_recv()
    dh_relay.wait_recv()

    head_dim = wk_ref.shape[1]
    d_hid = jnp.concatenate([dh_all[s] for s in range(n_ep)], axis=0)
    d_attn = dot_nt(d_hid, wo_ref[...]).astype(BF16)
    d_q, d_k, d_v = [], [], []
    for s in range(n_ep):
        rows = slice(s * seq_len, (s + 1) * seq_len)
        d_out = stack_heads(d_attn[rows], heads, head_dim)
        probs = p_ref[s]
        d_probs = dot_nt(d_out, v_ref[rows, :])
        d_v.append(dot_tn(probs.astype(BF16), d_out).astype(BF16))
        d_scores = (probs * (d_probs - jnp.sum(probs * d_probs, axis=-1, keepdims=True)) * head_dim ** -0.5).astype(BF16)
        d_q.append(unstack_heads(dot_nn(d_scores, k_ref[rows, :]).astype(BF16), heads, seq_len))
        d_k.append(dot_tn(d_scores, stack_heads(q_ref[rows, :], heads, head_dim)).astype(BF16))
    d_q, d_k, d_v = [jnp.concatenate(part, axis=0) for part in (d_q, d_k, d_v)]
    d_norm1 = dot_nt(d_q, wq_s[...]) + dot_nt(d_k, wk_ref[...]) + dot_nt(d_v, wv_ref[...])
    x_f32 = jnp.concatenate([x_ref[s] for s in range(n_ep)], axis=0).astype(F32)
    inv1 = rms_inv(x_f32)
    x_hat = x_f32 * inv1
    d_hat1 = d_norm1 * gain1
    d_x = inv1 * (d_hat1 - x_hat * jnp.mean(d_hat1 * x_hat, axis=-1, keepdims=True)) + d_hid.astype(F32)
    dx_all[...] = d_x.astype(BF16)
    dx_c = push(dx_all.at[mine], dx_ref, sems, 11, {'pp': earlier})
    dx_c.start()
    dg1_ref[...] = jnp.sum(d_norm1 * x_hat, axis=0, keepdims=True)

    near_a_c.wait_recv()
    far_a_c.wait_recv()
    y_own[...] = (ha_ref[mine, :].astype(F32) + (ra_ref[me] + near_a[...] + far_a[...])).astype(BF16)
    y_c = push(y_own, y_ref, sems, 12, {'pp': later})
    y_c.start()
    normed = n1_ref[...]
    d_w_q = dot_tn(normed, d_q)
    for h in range(heads):
        dwq_ref[h] = d_w_q[:, h * LANES:(h + 1) * LANES]
    dwk_ref[...] = dot_tn(normed, d_k)
    dwv_ref[...] = dot_tn(normed, d_v)
    dwo_ref[...] = dot_tn(o_ref[...], d_hid)
    small_far.wait_recv()
    sums = small_2[...] + small_3[...]
    dwr_ref[...] = sums[0:8, :]
    dg2_ref[...] = sums[8:9, :]
    dx_c.wait_recv()
    y_c.wait_recv()
    for copy in (swap_b_c, near_b_c, swap_a_c, near_a_c, far_b_c, far_a_c, dh_far, dh_near, dh_relay, small_near, small_far,
                 dx_c, y_c):
        copy.wait_send()


def shape_of(shape, dtype):
    return jax.ShapeDtypeStruct(shape, dtype)


def solution(mesh):
    n_ep, n_pp = mesh.shape['ep'], mesh.shape['pp']
    whole = pl.BlockSpec(memory_space=VMEM)

    def device_tick(x_a, x_b, g_b, ids_a, ids_b, count_a, count_b, gain_1, gain_2, w_q, w_k, w_v, w_o, w_r, w_1, w_3, w_2):
        seq_len, d_model = x_a.shape[2], x_a.shape[3]
        heads, head_dim = w_q.shape[2], w_q.shape[3]
        n_exp, e_local, ffn = w_r.shape[2], w_1.shape[1], w_1.shape[3]
        n_tok = n_ep * seq_len
        width = heads * head_dim
        xa, xb, gb = x_a[0, 0], x_b[0, 0], g_b[0, 0]
        wq = jnp.transpose(w_q[0], (1, 0, 2))
        wk, wv, wo = w_k[0, :, 0], w_v[0, :, 0], w_o[0].reshape(width, d_model)
        wr = jnp.transpose(w_r[0])
        packed = jnp.concatenate([
            ids_a[0, 0].T, ids_b[0, 0].T, jnp.pad(count_a[0], ((0, 0), (0, LANES - n_exp))),
            jnp.pad(count_b[0], ((0, 0), (0, LANES - n_exp))), jnp.zeros((2, LANES), jnp.int32)], axis=0)
        tok, rows = (n_ep, seq_len, d_model), (n_tok, d_model)
        head_out = [shape_of(tok, BF16), shape_of(tok, BF16), shape_of(rows, BF16), shape_of(rows, BF16),
                    shape_of((n_tok, LANES), F32), shape_of((n_tok, LANES), F32), shape_of((n_tok, LANES), F32),
                    shape_of((n_tok, LANES), F32), shape_of((n_tok, LANES), F32), shape_of(rows, BF16), shape_of(rows, BF16),
                    shape_of(rows, BF16), shape_of((n_tok, width), BF16), shape_of((n_tok, head_dim), BF16),
                    shape_of((n_tok, head_dim), BF16), shape_of((n_ep, heads * seq_len, seq_len), F32),
                    shape_of((n_tok, width), BF16)]
        (xb_all, gb_all, n2a, n2b, wta, m_a, wtb, m_b, rtb, ha, hb, n1, q, k, v, probs, attn) = pl.pallas_call(
            functools.partial(head_kernel, n_ep, heads),
            out_shape=head_out,
            in_specs=[whole] * 11,
            out_specs=[whole] * len(head_out),
            scratch_shapes=[VMEM(tok, BF16), VMEM((n_ep, 8, LANES), jnp.int32), VMEM((d_model, width), BF16),
                            VMEM((LANES, d_model), BF16), pltpu.SemaphoreType.DMA((12,)), pltpu.SemaphoreType.DMA((12,))],
            compiler_params=pltpu.CompilerParams(collective_id=0, has_side_effects=True, vmem_limit_bytes=60 * 2 ** 20),
            name='head',
        )(packed, xa, xb, gb, gain_1, gain_2, wq, wk, wv, wo, wr)

        n_tile = ffn // FFN_TILE

        def const(*shape):
            return pl.BlockSpec(shape, lambda e, f: (0,) * len(shape))
        in_tile = pl.BlockSpec((1, d_model, FFN_TILE), lambda e, f: (e, 0, f))
        out_tile = pl.BlockSpec((1, FFN_TILE, d_model), lambda e, f: (e, f, 0))
        r_a, r_b, dw1, dw3, dw2 = pl.pallas_call(
            functools.partial(moe_kernel, e_local),
            grid=(e_local, n_tile),
            out_shape=[shape_of(rows, F32), shape_of((n_tok, d_model + LANES), F32), shape_of((e_local, d_model, ffn), F32),
                       shape_of((e_local, d_model, ffn), F32), shape_of((e_local, ffn, d_model), F32)],
            in_specs=[const(*rows)] * 3 + [const(n_tok, LANES)] * 4 + [in_tile, in_tile, out_tile],
            out_specs=[const(*rows), const(n_tok, d_model + LANES), in_tile, in_tile, out_tile],
            scratch_shapes=[VMEM((2 * n_tok, d_model), BF16), VMEM((d_model, n_tok), BF16), VMEM(rows, BF16),
                            VMEM((2 * n_tok, d_model), F32), VMEM(rows, F32), VMEM((3, n_tok, LANES), F32)],
            compiler_params=pltpu.CompilerParams(dimension_semantics=('arbitrary', 'arbitrary'),
                                                 vmem_limit_bytes=60 * 2 ** 20),
            name='moe',
        )(n2a, n2b, gb_all.reshape(rows), wta, m_a, wtb, m_b, w_1[0], w_3[0], w_2[0])

        small = (16, d_model)
        block, wide = (seq_len, d_model), (seq_len, d_model + LANES)
        y_next, dx_prev, dwq, dwk, dwv, dwo, dg1, dg2, dwr = pl.pallas_call(
            functools.partial(tail_kernel, n_ep, n_pp, heads),
            out_shape=[shape_of(block, BF16), shape_of(block, BF16), shape_of((heads, d_model, head_dim), F32),
                       shape_of((d_model, head_dim), F32), shape_of((d_model, head_dim), F32), shape_of((width, d_model), F32),
                       shape_of((1, d_model), F32), shape_of((1, d_model), F32), shape_of((n_exp, d_model), F32)],
            in_specs=[whole] * 21,
            out_specs=[whole] * 9,
            scratch_shapes=[VMEM(wide, F32)] * 4 + [VMEM(block, F32)] * 4 + [VMEM(tok, BF16)] + [VMEM(small, F32)] * 4
            + [VMEM(block, BF16), VMEM(rows, BF16), VMEM((d_model, width), BF16), VMEM((LANES, d_model), BF16),
               pltpu.SemaphoreType.DMA((13,)), pltpu.SemaphoreType.DMA((13,))],
            compiler_params=pltpu.CompilerParams(collective_id=1, has_side_effects=True, vmem_limit_bytes=60 * 2 ** 20),
            name='tail',
        )(r_a.reshape(tok), r_b.reshape((n_ep,) + wide), ha, hb, n2b, gb_all, rtb, xb_all, n1, q, k, v, probs, attn,
          gain_1, gain_2, wq, wk, wv, wo, wr)
        return (y_next[None, None], dx_prev[None, None], dg1, dg2, jnp.transpose(dwq, (1, 0, 2))[None], dwk[None, :, None],
                dwv[None, :, None], dwo.reshape(w_o.shape), jnp.transpose(dwr)[None], dw1[None], dw3[None], dw2[None])

    tok_spec = P(('dp', 'pp'), 'ep', None, None)
    cnt_spec = P(('dp', 'pp'), 'ep', None)
    gain_spec = P('pp', None)
    attn_spec = P('pp', None, None, None)
    router_spec = P('pp', None, None)
    expert_spec = P('pp', 'ep', None, None)
    gain_out = P(('dp', 'pp'), None)
    attn_out_spec = P(('dp', 'pp'), None, None, None)
    router_out = P(('dp', 'pp'), None, None)
    expert_out_spec = P(('dp', 'pp'), 'ep', None, None)
    in_specs = (tok_spec, tok_spec, tok_spec, tok_spec, tok_spec, cnt_spec, cnt_spec, gain_spec, gain_spec,
                attn_spec, attn_spec, attn_spec, attn_spec, router_spec, expert_spec, expert_spec, expert_spec)
    out_specs = (tok_spec, tok_spec, gain_out, gain_out, attn_out_spec, attn_out_spec, attn_out_spec, attn_out_spec,
                 router_out, expert_out_spec, expert_out_spec, expert_out_spec)
    return jax.shard_map(device_tick, mesh=mesh, in_specs=in_specs, out_specs=out_specs, check_vma=False)
```

time: 409 us -> 154 us (0.38); the launches traced: 402 us -> 153 us
  Pallas kernels: 0 us -> 137 us
  matrix products: 134 us -> 0 us
  waiting for transfers between devices: 67.2 us -> 0 us
  local copies, waits for them, and re-layouts: 82.2 us -> 15.3 us
  other arithmetic: 54.9 us -> 0 us
  starting transfers between devices: 35.9 us -> 0 us
  between operations: 15.6 us -> 0.67 us
  blocking collectives: 12.3 us -> 0 us
    pallas_call x0 -> x3, Pallas kernels: none -> 137 us  [the longest x1 61.5 us: device_tick(): pl.pallas_call(functools.partial(moe_kernel, e_local), grid=(e_local, n_t...]
    dot_general x38 -> x0, matrix products: 134 us -> none  [the longest x2 22.2 us: moe_forward(): jnp.einsum('secd,edf->secf', recv_buf, w_1, preferred_element_type=jnp.fl...]
    all_to_all x6 -> x0, waiting for transfers between devices: 58.3 us -> none  [exchange(): return lax.all_to_all(send_block, 'ep', 0, 0, tiled=True)]
    gather x9 -> x0, local copies, waits for them, and re-layouts: 37.7 us -> none  [the longest x2 10.4 us: moe_forward(): jnp.take(normed, choice_idx // top_k, axis=0)]
    all_to_all x6 -> x0, starting transfers between devices: 26.8 us -> none  [exchange(): return lax.all_to_all(send_block, 'ep', 0, 0, tiled=True)]
    reduce_sum x15 -> x0, other arithmetic: 14.4 us -> none  [the longest x1 2.34 us: moe_backward(): jnp.sum(jnp.where(keep_tk[:, :, None], d_picked.astype(jnp.float32), 0.0)...]
    gather x8 -> x0, other arithmetic: 13.3 us -> none  [the longest x4 10.3 us: routing_plan(): keep_mask = rank_idx < counts[ids_flat]]
    psum x1 -> x0, blocking collectives: 12.3 us -> none  [device_tick(): lax.psum((d_gain_1, d_gain_2, d_w_q, d_w_k, d_w_v, d_w_o, d_w_r), 'ep')]
  transfers between devices with their start and end apart: 9 -> 0, of which waited for: 6 -> 0; matrix products, arithmetic and copies ran while one was open for 30% -> 0% of each run, Pallas kernels for 0% -> 0%
where the time goes in v1:
time: 154 us; the launch traced here: 153 us
  Pallas kernels  137 us (89%)
  local copies, waits for them, and re-layouts  15.3 us (10%)
    pallas_call x1, Pallas kernels, device_tick(): pl.pallas_call(functools.partial(moe_kernel, e_local), grid=(e_local, n_t...  61.5 us
    pallas_call x1, Pallas kernels, device_tick(): pl.pallas_call(functools.partial(tail_kernel, n_ep, n_pp, heads), out_sha...  49.2 us
    pallas_call x1, Pallas kernels, device_tick(): pl.pallas_call(functools.partial(head_kernel, n_ep, heads), out_shape=hea...  26.7 us
    unnamed x17, local copies, waits for them, and re-layouts  12.6 us

profile of v1, /device:TPU:0, one launch (start us, length us, event | category | flops | bytes accessed | tf_op | source)
XLA Modules:
  0.0 153.3 jit_solution(11072787758058956839)
XLA Ops:
  0.6 0.7 pad.7
  1.3 0.7 pad.8
  2.0 1.3 concatenate.3.pk_ref
  3.3 26.7 %head.1 = (bf16[4,128,768]{2,1,0:T(8,128)(2,1)}, bf16[4,128,768]{2,1,0:T(8,128)(2,1)}, bf16[512,768]{1,0:T(8,128)(2,1)}, bf16[512,768]{1,0:T(8,128)(2,1)}, f32[5...) custom-call(s32[8,128]{1,0:T(8,128)} %concatenate.3.pk_ref, ...), custom_call_target="tpu_custom_call" | custom-call | tf_op jit(solution)/shard_map/head/pallas_call | solution.py:389
  29.9 61.5 %moe.1 = (f32[512,768]{1,0:T(8,128)}, f32[512,896]{1,0:T(8,128)}, f32[2,768,2048]{2,1,0:T(8,128)}, f32[2,768,2048]{2,1,0:T(8,128)}, f32[2,2048,768]{2,1,0:T(8,128)}) custom-call(bf16[512,768]{1,0:T(8,128)(2,1)} %get-tuple-element.43.n2a_ref, bf16[512,768]{1,0:T(8,128)(2,1)} %get-tuple-element.44.n2b_ref, bf16[512,768]{1,0:T(8,128)(2,1)} %bitcast.51, ...), custom_call_target="tpu_custom_call" | custom-call | tf_op jit(solution)/shard_map/moe/pallas_call | solution.py:406
  91.4 49.2 %tail.1 = (bf16[128,768]{1,0:T(8,128)(2,1)}, bf16[128,768]{1,0:T(8,128)(2,1)}, f32[6,768,128]{2,1,0:T(8,128)}, f32[768,128]{1,0:T(8,128)}, f32[768,128]{1,0:T(8,...) custom-call(f32[4,128,768]{2,1,0:T(8,128)} %bitcast.55, ...), custom_call_target="tpu_custom_call" | custom-call | tf_op jit(solution)/shard_map/tail/pallas_call | solution.py:422
  140.6 1.6 %copy.40 = bf16[1,1,128,768]{3,2,1,0:T(8,128)(2,1)} copy(bf16[1,1,128,768]{3,2,1,0:T(8,128)(2,1)} %bitcast.66) | data formatting | bytes 393216
  142.3 1.6 %copy.41 = bf16[1,1,128,768]{3,2,1,0:T(8,128)(2,1)} copy(bf16[1,1,128,768]{3,2,1,0:T(8,128)(2,1)} %bitcast.65) | data formatting | bytes 393216
  143.9 1.3 copy.42
  145.1 1.2 copy.43
  146.4 0.0 copy-start.2
  146.4 0.0 copy-start.1
  146.4 0.0 copy-start
  146.4 3.4 %copy.44 = f32[1,768,6,128]{3,1,2,0:T(8,128)} copy(f32[1,768,6,128]{3,1,2,0:T(8,128)} %bitcast.53) | data formatting | bytes 4718592
  149.8 0.0 copy-done.2
  149.8 0.7 copy.45
  150.5 0.0 copy-done.1
  150.5 0.7 copy.46
  151.3 0.0 copy-done
  151.3 0.0 copy-start.3
  151.3 1.4 copy.47
  152.7 0.0 copy-done.3
  152.7 0.6 copy.48
  (1 shorter events, 0.0 us)
Async XLA Ops:
  146.4 3.4 %copy-start.2 = (f32[768,128]{1,0:T(8,128)S(1)}, f32[768,128]{1,0:T(8,128)}, u32[]{:S(2)}) copy-start(f32[768,128]{1,0:T(8,128)} %get-tuple-element.67) | copy-start | bytes 1179652
  146.4 4.1 %copy-start.1 = (f32[768,128]{1,0:T(8,128)S(1)}, f32[768,128]{1,0:T(8,128)}, u32[]{:S(2)}) copy-start(f32[768,128]{1,0:T(8,128)} %get-tuple-element.68) | copy-start | bytes 1179652
  146.4 4.9 %copy-start = (f32[768,768]{1,0:T(8,128)S(1)}, f32[768,768]{1,0:T(8,128)}, u32[]{:S(2)}) copy-start(f32[768,768]{1,0:T(8,128)} %get-tuple-element.69) | copy-start | bytes 7077892
  151.3 1.4 copy-start.3

commit v2 on v1

--- a/solution.py
+++ b/solution.py
@@ -15,6 +15,10 @@
 VMEM = pltpu.VMEM
 FFN_TILE = 256
 LANES = 128
+HEAD_VMEM = 34 * 2 ** 20
+MOE_VMEM = 44 * 2 ** 20
+TAIL_VMEM = 30 * 2 ** 20
+DENSE_VMEM = 24 * 2 ** 20
 
 
 def dot_nn(lhs, rhs):
@@ -118,13 +122,17 @@
     return normed, jnp.concatenate(weights, 0), jnp.concatenate(masks, 0), jnp.concatenate(routes, 0)
 
 
-def head_kernel(n_ep, heads, pk_ref, xa_ref, xb_ref, gb_ref, gain1_ref, gain2_ref, wq_ref, wk_ref, wv_ref, wo_ref, wr_ref,
+def head_kernel(n_ep, heads, ida_ref, idb_ref, cta_ref, ctb_ref, xa_ref, xb_ref, gb_ref, gain1_ref, gain2_ref, wq_ref, wk_ref, wv_ref, wo_ref, wr_ref,
                 xb_all, gb_all, n2a_ref, n2b_ref, wta_ref, ma_ref, wtb_ref, mb_ref, rtb_ref, ha_ref, hb_ref,
                 n1_ref, q_ref, k_ref, v_ref, p_ref, o_ref,
-                xa_all, pk_all, wq_s, wr_s, send_sem, recv_sem):
+                xa_all, pk_ref, pk_all, wq_s, wr_s, send_sem, recv_sem):
     me, partner, across, diag = ep_peers()
-    seq_len = xa_ref.shape[0]
     sems = (send_sem, recv_sem)
+    pk_ref[...] = jnp.zeros_like(pk_ref)
+    pk_ref[0:2, :] = ida_ref[...]
+    pk_ref[2:4, :] = idb_ref[...]
+    pk_ref[4:5, 0:cta_ref.shape[1]] = cta_ref[...]
+    pk_ref[5:6, 0:ctb_ref.shape[1]] = ctb_ref[...]
     greet(({'ep': partner}, {'ep': across}))
     own, landing = (pk_ref, xb_ref, xa_ref, gb_ref), (pk_all, xb_all, xa_all, gb_all)
     near, far, relay = [], [], []
@@ -238,11 +246,11 @@
         rb_ref[:, d_model:] += jnp.where(lane == here, pick, 0.0)
 
 
-def tail_kernel(n_ep, n_pp, heads, ra_ref, rb_ref, ha_ref, hb_ref, n2b_ref, gb_ref, rtb_ref, x_ref, n1_ref, q_ref, k_ref, v_ref,
-                p_ref, o_ref, gain1_ref, gain2_ref, wq_ref, wk_ref, wv_ref, wo_ref, wr_ref,
-                y_ref, dx_ref, dwq_ref, dwk_ref, dwv_ref, dwo_ref, dg1_ref, dg2_ref, dwr_ref,
-                near_b, swap_b, sum_b, far_b, near_a, swap_a, sum_a, far_a, dh_all, small, small_1, small_2, small_3,
-                y_own, dx_all, wq_s, wr_s, send_sem, recv_sem):
+def tail_kernel(n_ep, n_pp, heads, ra_ref, rb_ref, ha_ref, hb_ref, n2b_ref, gb_ref, rtb_ref, x_ref, q_ref, k_ref, v_ref,
+                p_ref, gain1_ref, gain2_ref, wq_ref, wk_ref, wv_ref, wo_ref, wr_ref,
+                y_ref, dx_ref, dq_ref, dk_ref, dv_ref, dh_all, dg1_ref, sums_ref,
+                near_b, swap_b, sum_b, far_b, near_a, swap_a, sum_a, far_a, small, small_1, small_2, small_3,
+                y_own, dx_own, wq_s, wr_s, send_sem, recv_sem):
     me, partner, across, diag = ep_peers()
     stage = lax.axis_index('pp')
     later, earlier = lax.rem(stage + 1, n_pp), lax.rem(stage + n_pp - 1, n_pp)
@@ -300,62 +308,79 @@
     small[8:16, :] = jnp.broadcast_to(jnp.sum(d_normed * h_hat, axis=0, keepdims=True), (8, d_model))
     small_near = push(small, small_1, sems, 9, near)
     small_near.start()
+
+    head_dim = wk_ref.shape[1]
+
+    def attention_back(s):
+        rows = pl.ds(pl.multiple_of(s * seq_len, seq_len), seq_len)
+        d_hid = dh_all[s]
+        d_out = stack_heads(dot_nt(d_hid, wo_ref[...]).astype(BF16), heads, head_dim)
+        probs = p_ref[s]
+        d_probs = dot_nt(d_out, v_ref[rows, :])
+        d_v = dot_tn(probs.astype(BF16), d_out).astype(BF16)
+        d_scores = (probs * (d_probs - jnp.sum(probs * d_probs, axis=-1, keepdims=True)) * head_dim ** -0.5).astype(BF16)
+        d_q = unstack_heads(dot_nn(d_scores, k_ref[rows, :]).astype(BF16), heads, seq_len)
+        d_k = dot_tn(d_scores, stack_heads(q_ref[rows, :], heads, head_dim)).astype(BF16)
+        dq_ref[rows, :], dk_ref[rows, :], dv_ref[rows, :] = d_q, d_k, d_v
+        d_norm1 = dot_nt(d_q, wq_s[...]) + dot_nt(d_k, wk_ref[...]) + dot_nt(d_v, wv_ref[...])
+        x_f32 = x_ref[s].astype(F32)
+        inv1 = rms_inv(x_f32)
+        x_hat = x_f32 * inv1
+        dg1_ref[s] = jnp.broadcast_to(jnp.sum(d_norm1 * x_hat, axis=0, keepdims=True), (8, d_model))
+        return d_hid, d_norm1, inv1, x_hat
+
+    d_hid, d_norm1, inv1, x_hat = attention_back(me)
+    d_hat1 = d_norm1 * gain1
+    d_x = inv1 * (d_hat1 - x_hat * jnp.mean(d_hat1 * x_hat, axis=-1, keepdims=True)) + d_hid.astype(F32)
+    dx_own[...] = d_x.astype(BF16)
+    dx_c = push(dx_own, dx_ref, sems, 11, {'pp': earlier})
+    dx_c.start()
     small_near.wait_recv()
     small_2[...] = small[...] + small_1[...]
     small_far = push(small_2, small_3, sems, 10, over)
     small_far.start()
     far_a_c.start()
+    dh_near.wait_recv()
+    attention_back(partner)
     dh_far.wait_recv()
     dh_relay.start()
-    dh_near.wait_recv()
+    attention_back(across)
     dh_relay.wait_recv()
-
-    head_dim = wk_ref.shape[1]
-    d_hid = jnp.concatenate([dh_all[s] for s in range(n_ep)], axis=0)
-    d_attn = dot_nt(d_hid, wo_ref[...]).astype(BF16)
-    d_q, d_k, d_v = [], [], []
-    for s in range(n_ep):
-        rows = slice(s * seq_len, (s + 1) * seq_len)
-        d_out = stack_heads(d_attn[rows], heads, head_dim)
-        probs = p_ref[s]
-        d_probs = dot_nt(d_out, v_ref[rows, :])
-        d_v.append(dot_tn(probs.astype(BF16), d_out).astype(BF16))
-        d_scores = (probs * (d_probs - jnp.sum(probs * d_probs, axis=-1, keepdims=True)) * head_dim ** -0.5).astype(BF16)
-        d_q.append(unstack_heads(dot_nn(d_scores, k_ref[rows, :]).astype(BF16), heads, seq_len))
-        d_k.append(dot_tn(d_scores, stack_heads(q_ref[rows, :], heads, head_dim)).astype(BF16))
-    d_q, d_k, d_v = [jnp.concatenate(part, axis=0) for part in (d_q, d_k, d_v)]
-    d_norm1 = dot_nt(d_q, wq_s[...]) + dot_nt(d_k, wk_ref[...]) + dot_nt(d_v, wv_ref[...])
-    x_f32 = jnp.concatenate([x_ref[s] for s in range(n_ep)], axis=0).astype(F32)
-    inv1 = rms_inv(x_f32)
-    x_hat = x_f32 * inv1
-    d_hat1 = d_norm1 * gain1
-    d_x = inv1 * (d_hat1 - x_hat * jnp.mean(d_hat1 * x_hat, axis=-1, keepdims=True)) + d_hid.astype(F32)
-    dx_all[...] = d_x.astype(BF16)
-    dx_c = push(dx_all.at[mine], dx_ref, sems, 11, {'pp': earlier})
-    dx_c.start()
-    dg1_ref[...] = jnp.sum(d_norm1 * x_hat, axis=0, keepdims=True)
+    attention_back(diag)
 
     near_a_c.wait_recv()
     far_a_c.wait_recv()
     y_own[...] = (ha_ref[mine, :].astype(F32) + (ra_ref[me] + near_a[...] + far_a[...])).astype(BF16)
     y_c = push(y_own, y_ref, sems, 12, {'pp': later})
     y_c.start()
-    normed = n1_ref[...]
-    d_w_q = dot_tn(normed, d_q)
-    for h in range(heads):
-        dwq_ref[h] = d_w_q[:, h * LANES:(h + 1) * LANES]
-    dwk_ref[...] = dot_tn(normed, d_k)
-    dwv_ref[...] = dot_tn(normed, d_v)
-    dwo_ref[...] = dot_tn(o_ref[...], d_hid)
     small_far.wait_recv()
-    sums = small_2[...] + small_3[...]
-    dwr_ref[...] = sums[0:8, :]
-    dg2_ref[...] = sums[8:9, :]
+    sums_ref[...] = small_2[...] + small_3[...]
     dx_c.wait_recv()
     y_c.wait_recv()
     for copy in (swap_b_c, near_b_c, swap_a_c, near_a_c, far_b_c, far_a_c, dh_far, dh_near, dh_relay, small_near, small_far,
                  dx_c, y_c):
         copy.wait_send()
+
+
+def dense_kernel(n1_ref, o_ref, dq_ref, dk_ref, dv_ref, dh_ref, dg1_in, sums_in, y_in, dx_in,
+                 dwq_ref, dwk_ref, dwv_ref, dwo_ref, dg1_ref, dg2_ref, dwr_ref, y_ref, dx_ref, n1t):
+    step = pl.program_id(0)
+
+    @pl.when(step == 0)
+    def _():
+        n1t[...] = n1_ref[...].astype(F32).T.astype(BF16)
+        dwk_ref[...] = dot_nn(n1t[...], dk_ref[...])
+        dwv_ref[...] = dot_nn(n1t[...], dv_ref[...])
+        dg1_ref[...] = sum(dg1_in[s] for s in range(dg1_in.shape[0]))[0:1]
+        dwr_ref[...] = sums_in[0:8, :]
+        dg2_ref[...] = sums_in[8:9, :]
+        y_ref[...] = y_in[...]
+        dx_ref[...] = dx_in[...]
+
+    pair = dot_nn(n1t[...], dq_ref[...])
+    for i in range(dwq_ref.shape[0]):
+        dwq_ref[i] = pair[:, i * LANES:(i + 1) * LANES]
+    dwo_ref[...] = dot_tn(o_ref[...], dh_ref[...])
 
 
 def shape_of(shape, dtype):
@@ -376,9 +401,6 @@
         wq = jnp.transpose(w_q[0], (1, 0, 2))
         wk, wv, wo = w_k[0, :, 0], w_v[0, :, 0], w_o[0].reshape(width, d_model)
         wr = jnp.transpose(w_r[0])
-        packed = jnp.concatenate([
-            ids_a[0, 0].T, ids_b[0, 0].T, jnp.pad(count_a[0], ((0, 0), (0, LANES - n_exp))),
-            jnp.pad(count_b[0], ((0, 0), (0, LANES - n_exp))), jnp.zeros((2, LANES), jnp.int32)], axis=0)
         tok, rows = (n_ep, seq_len, d_model), (n_tok, d_model)
         head_out = [shape_of(tok, BF16), shape_of(tok, BF16), shape_of(rows, BF16), shape_of(rows, BF16),
                     shape_of((n_tok, LANES), F32), shape_of((n_tok, LANES), F32), shape_of((n_tok, LANES), F32),
@@ -389,13 +411,13 @@
         (xb_all, gb_all, n2a, n2b, wta, m_a, wtb, m_b, rtb, ha, hb, n1, q, k, v, probs, attn) = pl.pallas_call(
             functools.partial(head_kernel, n_ep, heads),
             out_shape=head_out,
-            in_specs=[whole] * 11,
+            in_specs=[whole] * 14,
             out_specs=[whole] * len(head_out),
-            scratch_shapes=[VMEM(tok, BF16), VMEM((n_ep, 8, LANES), jnp.int32), VMEM((d_model, width), BF16),
+            scratch_shapes=[VMEM(tok, BF16), VMEM((8, LANES), jnp.int32), VMEM((n_ep, 8, LANES), jnp.int32), VMEM((d_model, width), BF16),
                             VMEM((LANES, d_model), BF16), pltpu.SemaphoreType.DMA((12,)), pltpu.SemaphoreType.DMA((12,))],
-            compiler_params=pltpu.CompilerParams(collective_id=0, has_side_effects=True, vmem_limit_bytes=60 * 2 ** 20),
+            compiler_params=pltpu.CompilerParams(collective_id=0, has_side_effects=True, vmem_limit_bytes=HEAD_VMEM),
             name='head',
-        )(packed, xa, xb, gb, gain_1, gain_2, wq, wk, wv, wo, wr)
+        )(ids_a[0, 0].T, ids_b[0, 0].T, count_a[0], count_b[0], xa, xb, gb, gain_1, gain_2, wq, wk, wv, wo, wr)
 
         n_tile = ffn // FFN_TILE
 
@@ -413,26 +435,48 @@
             scratch_shapes=[VMEM((2 * n_tok, d_model), BF16), VMEM((d_model, n_tok), BF16), VMEM(rows, BF16),
                             VMEM((2 * n_tok, d_model), F32), VMEM(rows, F32), VMEM((3, n_tok, LANES), F32)],
             compiler_params=pltpu.CompilerParams(dimension_semantics=('arbitrary', 'arbitrary'),
-                                                 vmem_limit_bytes=60 * 2 ** 20),
+                                                 vmem_limit_bytes=MOE_VMEM),
             name='moe',
         )(n2a, n2b, gb_all.reshape(rows), wta, m_a, wtb, m_b, w_1[0], w_3[0], w_2[0])
 
         small = (16, d_model)
         block, wide = (seq_len, d_model), (seq_len, d_model + LANES)
-        y_next, dx_prev, dwq, dwk, dwv, dwo, dg1, dg2, dwr = pl.pallas_call(
+        y_in, dx_in, dq, dk, dv, dh, dg1_in, sums = pl.pallas_call(
             functools.partial(tail_kernel, n_ep, n_pp, heads),
-            out_shape=[shape_of(block, BF16), shape_of(block, BF16), shape_of((heads, d_model, head_dim), F32),
-                       shape_of((d_model, head_dim), F32), shape_of((d_model, head_dim), F32), shape_of((width, d_model), F32),
-                       shape_of((1, d_model), F32), shape_of((1, d_model), F32), shape_of((n_exp, d_model), F32)],
-            in_specs=[whole] * 21,
-            out_specs=[whole] * 9,
-            scratch_shapes=[VMEM(wide, F32)] * 4 + [VMEM(block, F32)] * 4 + [VMEM(tok, BF16)] + [VMEM(small, F32)] * 4
-            + [VMEM(block, BF16), VMEM(rows, BF16), VMEM((d_model, width), BF16), VMEM((LANES, d_model), BF16),
+            out_shape=[shape_of(block, BF16), shape_of(block, BF16), shape_of((n_tok, width), BF16),
+                       shape_of((n_tok, head_dim), BF16), shape_of((n_tok, head_dim), BF16), shape_of(tok, BF16),
+                       shape_of((n_ep, 8, d_model), F32), shape_of(small, F32)],
+            in_specs=[whole] * 19,
+            out_specs=[whole] * 8,
+            scratch_shapes=[VMEM(wide, F32)] * 4 + [VMEM(block, F32)] * 4 + [VMEM(small, F32)] * 4
+            + [VMEM(block, BF16), VMEM(block, BF16), VMEM((d_model, width), BF16), VMEM((LANES, d_model), BF16),
                pltpu.SemaphoreType.DMA((13,)), pltpu.SemaphoreType.DMA((13,))],
-            compiler_params=pltpu.CompilerParams(collective_id=1, has_side_effects=True, vmem_limit_bytes=60 * 2 ** 20),
+            compiler_params=pltpu.CompilerParams(collective_id=1, has_side_effects=True, vmem_limit_bytes=TAIL_VMEM),
             name='tail',
-        )(r_a.reshape(tok), r_b.reshape((n_ep,) + wide), ha, hb, n2b, gb_all, rtb, xb_all, n1, q, k, v, probs, attn,
+        )(r_a.reshape(tok), r_b.reshape((n_ep,) + wide), ha, hb, n2b, gb_all, rtb, xb_all, q, k, v, probs,
           gain_1, gain_2, wq, wk, wv, wo, wr)
+
+        pair = 2
+        steps = heads // pair
+
+        def held(*shape):
+            return pl.BlockSpec(shape, lambda i: (0,) * len(shape))
+        cols = pl.BlockSpec((n_tok, pair * head_dim), lambda i: (0, i))
+        dwq, dwk, dwv, dwo, dg1, dg2, dwr, y_next, dx_prev = pl.pallas_call(
+            dense_kernel,
+            grid=(steps,),
+            out_shape=[shape_of((heads, d_model, head_dim), F32), shape_of((d_model, head_dim), F32),
+                       shape_of((d_model, head_dim), F32), shape_of((width, d_model), F32), shape_of((1, d_model), F32),
+                       shape_of((1, d_model), F32), shape_of((n_exp, d_model), F32), shape_of(block, BF16), shape_of(block, BF16)],
+            in_specs=[held(*rows), cols, cols, held(n_tok, head_dim), held(n_tok, head_dim), held(*rows),
+                      held(n_ep, 8, d_model), held(*small), held(*block), held(*block)],
+            out_specs=[pl.BlockSpec((pair, d_model, head_dim), lambda i: (i, 0, 0)), held(d_model, head_dim),
+                       held(d_model, head_dim), pl.BlockSpec((pair * head_dim, d_model), lambda i: (i, 0)),
+                       held(1, d_model), held(1, d_model), held(n_exp, d_model), held(*block), held(*block)],
+            scratch_shapes=[VMEM((d_model, n_tok), BF16)],
+            compiler_params=pltpu.CompilerParams(dimension_semantics=('arbitrary',), vmem_limit_bytes=DENSE_VMEM),
+            name='dense',
+        )(n1, attn, dq, dk, dv, dh.reshape(rows), dg1_in, sums, y_in, dx_in)
         return (y_next[None, None], dx_prev[None, None], dg1, dg2, jnp.transpose(dwq, (1, 0, 2))[None], dwk[None, :, None],
                 dwv[None, :, None], dwo.reshape(w_o.shape), jnp.transpose(dwr)[None], dw1[None], dw3[None], dw2[None])
 

time: 154 us -> 138 us (0.90)
  Pallas kernels: 137 us -> 125 us
  local copies, waits for them, and re-layouts: 15.3 us -> 12 us
    pallas_call x1, Pallas kernels: 49.2 us -> 40.8 us  [device_tick(): pl.pallas_call(functools.partial(tail_kernel, n_ep, n_pp, heads), out_sha...]
    pallas_call x1, Pallas kernels: 26.7 us -> 20.8 us  [device_tick(): pl.pallas_call(functools.partial(head_kernel, n_ep, heads), out_shape=hea...]
    pallas_call x0 -> x1, Pallas kernels: none -> 4.17 us  [device_tick(): pl.pallas_call(dense_kernel, grid=(steps,), out_shape=[shape_of((heads, d...]
    pallas_call x1, Pallas kernels: 61.5 us -> 59 us  [device_tick(): pl.pallas_call(functools.partial(moe_kernel, e_local), grid=(e_local, n_t...]
    unnamed x17 -> x42, local copies, waits for them, and re-layouts: 12.6 us -> 12 us
where the time goes in v2:
time: 138 us
  Pallas kernels  125 us (91%)
  local copies, waits for them, and re-layouts  12 us (9%)
    pallas_call x1, Pallas kernels, device_tick(): pl.pallas_call(functools.partial(moe_kernel, e_local), grid=(e_local, n_t...  59 us
    pallas_call x1, Pallas kernels, device_tick(): pl.pallas_call(functools.partial(tail_kernel, n_ep, n_pp, heads), out_sha...  40.8 us
    pallas_call x1, Pallas kernels, device_tick(): pl.pallas_call(functools.partial(head_kernel, n_ep, heads), out_shape=hea...  20.8 us
    unnamed x42, local copies, waits for them, and re-layouts  12 us
    pallas_call x1, Pallas kernels, device_tick(): pl.pallas_call(dense_kernel, grid=(steps,), out_shape=[shape_of((heads, d...  4.17 us

profile of v2, /device:TPU:0, one launch (start us, length us, event | category | flops | bytes accessed | tf_op | source)
XLA Modules:
  0.0 137.5 jit_solution(16879075256400798441)
XLA Ops:
  0.6 0.0 copy-start
  0.7 1.3 copy-done
  1.9 0.0 copy-start.2
  1.9 1.3 copy-done.2
  3.2 0.0 copy-start.4
  3.2 0.9 copy-done.4
  4.1 0.0 copy-start.6
  4.1 0.9 copy-done.6
  5.0 0.0 copy-start.8
  5.0 0.9 copy-done.8
  6.0 0.0 copy-start.9
  6.0 0.9 copy-done.9
  6.9 0.0 copy-start.10
  6.9 0.9 copy-done.10
  7.8 0.0 copy-start.11
  7.8 0.7 copy-done.11
  8.5 0.0 copy-start.13
  8.5 0.7 copy-done.13
  9.2 0.0 copy-start.15
  9.2 0.7 copy-done.15
  9.9 0.0 copy-start.17
  9.9 0.7 copy-done.17
  10.6 0.0 copy-start.18
  10.6 0.7 copy-done.18
  11.3 0.0 copy-start.19
  11.3 0.7 copy-done.19
  11.9 0.0 copy-start.20
  11.9 0.7 copy-done.20
  12.6 20.8 %head.1 = (bf16[4,128,768]{2,1,0:T(8,128)(2,1)S(1)}, bf16[4,128,768]{2,1,0:T(8,128)(2,1)S(1)}, bf16[512,768]{1,0:T(8,128)(2,1)S(1)}, bf16[512,768]{1,0:T(8,128)(...) custom-call(s32[2,128]{1,0:T(2,128)S(1)} %bitcast.62, ...), custom_call_target="tpu_custom_call" | custom-call | tf_op jit(solution)/shard_map/head/pallas_call | solution.py:411
  33.4 0.0 copy-start.1
  33.4 0.0 copy-start.3
  33.4 0.0 copy-start.5
  33.5 0.0 copy-start.7
  33.5 0.0 copy-start.12
  33.5 0.0 copy-start.14
  33.5 0.0 copy-start.16
  33.5 59.0 %moe.1 = (f32[512,768]{1,0:T(8,128)S(1)}, f32[512,896]{1,0:T(8,128)S(1)}, f32[2,768,2048]{2,1,0:T(8,128)}, f32[2,768,2048]{2,1,0:T(8,128)}, f32[2,2048,768]{2,1,0:T(8,128)}) custom-call(bf16[512,768]{1,0:T(8,128)(2,1)S(1)} %get-tuple-element.53.n2a_ref, bf16[512,768]{1,0:T(8,128)(2,1)S(1)} %get-tuple-element.54.n2b_ref, bf16[512,768]{1,0:T(8,128)(2,1)S(1)} %bitcast.49, ...), custom_call_target="tpu_custom_call" | custom-call | tf_op jit(solution)/shard_map/moe/pallas_call | solution.py:428
  92.5 0.0 copy-done.1
  92.5 0.0 copy-done.3
  92.5 0.0 copy-done.5
  92.5 0.0 copy-done.7
  92.5 0.0 copy-done.12
  92.5 0.0 copy-done.14
  92.5 0.0 copy-done.16
  92.5 40.8 %tail.1 = (bf16[128,768]{1,0:T(8,128)(2,1)S(1)}, bf16[128,768]{1,0:T(8,128)(2,1)S(1)}, bf16[512,768]{1,0:T(8,128)(2,1)S(1)}, bf16[512,128]{1,0:T(8,128)(2,1)S(1)...) custom-call(f32[4,128,768]{2,1,0:T(8,128)S(1)} %bitcast.51, ...), custom_call_target="tpu_custom_call" | custom-call | tf_op jit(solution)/shard_map/tail/pallas_call | solution.py:444
  133.3 4.2 %dense.1 = (f32[6,768,128]{2,1,0:T(8,128)}, f32[768,128]{1,0:T(8,128)}, f32[768,128]{1,0:T(8,128)}, f32[768,768]{1,0:T(8,128)}, f32[1,768]{1,0:T(1,128)}, /*inde...) custom-call(bf16[512,768]{1,0:T(8,128)(2,1)S(1)} %get-tuple-element.51.n1_ref, ...), custom_call_target="tpu_custom_call" | custom-call | tf_op jit(solution)/shard_map/dense/pallas_call | solution.py:465
Async XLA Ops:
  0.6 1.3 copy-start
  1.9 1.3 copy-start.2
  3.2 0.9 copy-start.4
  4.1 0.9 copy-start.6
  5.0 0.9 copy-start.8
  6.0 0.9 copy-start.9
  6.9 0.9 copy-start.10
  7.8 0.7 copy-start.11
  8.5 0.7 copy-start.13
  9.2 0.7 copy-start.15
  9.9 0.7 copy-start.17
  10.6 0.7 copy-start.18
  11.3 0.7 copy-start.19
  11.9 0.7 copy-start.20
  33.4 59.1 %copy-start.1 = (bf16[1,768,6,128]{3,1,2,0:T(8,128)(2,1)S(1)}, bf16[1,768,6,128]{3,1,2,0:T(8,128)(2,1)}, u32[]{:S(2)}) copy-start(bf16[1,768,6,128]{3,1,2,0:T(8,128)(2,1)} %param.26) | copy-start | bytes 3538948
  33.4 59.1 %copy-start.3 = (bf16[1,6,128,768]{3,2,1,0:T(8,128)(2,1)S(1)}, bf16[1,6,128,768]{3,2,1,0:T(8,128)(2,1)}, u32[]{:S(2)}) copy-start(bf16[1,6,128,768]{3,2,1,0:T(8,128)(2,1)} %param.29) | copy-start | bytes 3538948
  33.4 59.1 %copy-start.5 = (bf16[1,768,1,128]{3,1,2,0:T(8,128)(2,1)S(1)}, bf16[1,768,1,128]{3,1,2,0:T(8,128)(2,1)}, u32[]{:S(2)}) copy-start(bf16[1,768,1,128]{3,1,2,0:T(8,128)(2,1)} %param.27) | copy-start | bytes 589828
  33.5 59.0 %copy-start.7 = (bf16[1,768,1,128]{3,1,2,0:T(8,128)(2,1)S(1)}, bf16[1,768,1,128]{3,1,2,0:T(8,128)(2,1)}, u32[]{:S(2)}) copy-start(bf16[1,768,1,128]{3,1,2,0:T(8,128)(2,1)} %param.28) | copy-start | bytes 589828
  33.5 59.0 %copy-start.12 = (bf16[1,768,8]{1,2,0:T(8,128)(2,1)S(1)}, bf16[1,768,8]{1,2,0:T(8,128)(2,1)}, u32[]{:S(2)}) copy-start(bf16[1,768,8]{1,2,0:T(8,128)(2,1)} %param.30) | copy-start | bytes 36868
  33.5 59.0 %copy-start.14 = (bf16[1,768]{1,0:T(2,128)(2,1)S(1)}, bf16[1,768]{1,0:T(2,128)(2,1)}, u32[]{:S(2)}) copy-start(bf16[1,768]{1,0:T(2,128)(2,1)} %gain1_ref.3) | copy-start | bytes 4612
  33.5 59.0 %copy-start.16 = (bf16[1,768]{1,0:T(2,128)(2,1)S(1)}, bf16[1,768]{1,0:T(2,128)(2,1)}, u32[]{:S(2)}) copy-start(bf16[1,768]{1,0:T(2,128)(2,1)} %gain2_ref.3) | copy-start | bytes 4612
